TPU v7x, 32 devices: a whole 2x2x4 slice. The times are simulated.
32 devices in a mesh: blk: 16 (over z, y, core), row: 2 (over x).
Axes of the slice: x: 2, y: 2, z: 4, core: 2. Of those that a mesh axis runs over, the one named last changes fastest.
Arguments:
- features: float32 [2048, 256], P(('blk', 'row')), may hold values from -2 to 2, as said below
- probes: float32 [2048, 128], P(('blk', 'row')), may hold values from -6 to 6
- outputscale: float32 [1], replicated, may hold values from 0.05 to 0.2
- noise: float32 [1], replicated, may hold values from 0.5 to 2
- pivots: int32 [256], replicated, may hold values from 0 to 2047, as said below
Outputs:
- product: float32 [2048, 128], P(('blk', 'row'))
- preconditioned: float32 [2048, 128], P(('blk', 'row'))
Inputs may be any that keep to these rules, and one draw needn't show every extreme that they name: `pivots`: 256 distinct point indices. real-valued features.
All inputs are finite; a program needn't handle non-finite values.
Results may differ from a plain program's by a relative error of at most 0.0003.
Values sent between devices are 32-bit elements; how exact they have to be, the bound alone decides.
No kernel may reach another device: no remote copies, remote signals or barrier semaphores. Data moves between devices by JAX's collectives and lax.ppermute only.
A program may use at most 64 MiB of HBM per device.

v0:
```python
import jax
import jax.numpy as jnp
from jax import lax
from jax.sharding import PartitionSpec as P

STRIDE = 4


highest = lax.Precision.HIGHEST
root_five = 2.23606797749979


def shifted(block, axis, distance):
    devices = range(lax.axis_size(axis))
    route = [((i - distance) % len(devices), i) for i in devices]
    return lax.ppermute(block, axis, route)


def kernel_tile(row_feats, row_norms, col_feats, col_norms):
    inner = lax.dot_general(
        row_feats,
        col_feats,
        (((1,), (1,)), ((), ())),
        precision=highest,
        preferred_element_type=jnp.float32,
    )
    squared = jnp.maximum(row_norms[:, None] + col_norms[None, :] - 2.0 * inner, 0.0)
    scaled = root_five * jnp.sqrt(squared)
    return (1.0 + scaled + scaled * scaled / 3.0) * jnp.exp(-scaled)


def transposed_product(kernel_block, row_probes):
    return lax.dot_general(
        kernel_block,
        row_probes,
        (((0,), (0,)), ((), ())),
        precision=highest,
        preferred_element_type=jnp.float32,
    )


def quorum_members(block_count, spacing):
    half_count = block_count // 2
    members = list(range(spacing))
    reached = 0
    while reached < half_count:
        reached = reached + spacing
        members.append(reached % block_count)
    return members


def quorum_pairs(block_count, members):
    pair_list = []
    for offset in range(block_count // 2 + 1):
        chosen = None
        for lower_slot, lower_member in enumerate(members):
            for upper_slot, upper_member in enumerate(members):
                if chosen is None and (upper_member - lower_member) % block_count == offset:
                    chosen = (lower_slot, upper_slot)
        two_sided = offset != 0 and 2 * offset != block_count
        pair_list.append((chosen[0], chosen[1], two_sided))
    return pair_list


def member_sweep(fetched, fetched_norms, upper, lower_group, block_rows):
    local_rows, probe_count = fetched[upper][1].shape
    column_sums = jnp.zeros((block_rows, probe_count), jnp.float32)
    arrived_feats = lax.all_gather(fetched[upper][0], "row", axis=0, tiled=True)
    arrived_probes = lax.all_gather(fetched[upper][1], "row", axis=0, tiled=True)
    arrived_norms = jnp.sum(arrived_feats * arrived_feats, axis=1)
    updated = []
    for position, (lower, two_sided) in enumerate(lower_group):
        kernel_block = kernel_tile(
            fetched[lower][0], fetched_norms[lower], arrived_feats, arrived_norms
        )
        updated.append(
            jnp.dot(
                kernel_block, arrived_probes, precision=highest, preferred_element_type=jnp.float32
            )
        )
        if two_sided:
            current = column_sums
            column_sums = current + transposed_product(kernel_block, fetched[lower][1])
    return (tuple(updated), column_sums)


def per_device(features, probes, outputscale, noise, pivots):
    local_rows, probe_count = probes.shape
    block_count = lax.axis_size("blk")
    piece_count = lax.axis_size("row")
    piece_index = lax.axis_index("row")
    amplitude = outputscale[0]
    nugget = noise[0]
    members = quorum_members(block_count, STRIDE)
    pair_list = quorum_pairs(block_count, members)
    slot_count = len(members)
    block_rows = local_rows * piece_count
    own_norms = jnp.sum(features * features, axis=1)
    forward = [jnp.zeros((local_rows, probe_count), jnp.float32) for member in members]
    backward = [jnp.zeros((block_rows, probe_count), jnp.float32) for member in members]
    fetched = [(features, probes)]
    for member in members[1:]:
        fetched.append(shifted((features, probes), "blk", block_count - member))
    fetched_norms = [jnp.sum(entry[0] * entry[0], axis=1) for entry in fetched]
    for upper in range(slot_count):
        lower_group = [
            (lower, two_sided) for lower, target, two_sided in pair_list if target == upper
        ]
        partials, column_sums = member_sweep(fetched, fetched_norms, upper, lower_group, block_rows)
        for position, (lower, two_sided) in enumerate(lower_group):
            forward[lower] = forward[lower] + partials[position]
        backward[upper] = column_sums
    shared = lax.psum_scatter(jnp.stack(backward), "row", scatter_dimension=1, tiled=True)
    kernel_probes = forward[0] + shared[0]
    for position in range(1, slot_count):
        outgoing = forward[position] + shared[position]
        kernel_probes = kernel_probes + shifted(outgoing, "blk", members[position])
    product = amplitude * kernel_probes + nugget * probes
    flat_index = lax.axis_index("blk") * piece_count + piece_index
    offsets = pivots - flat_index * local_rows
    inside = (offsets >= 0) & (offsets < local_rows)
    picked = jnp.where(inside[:, None], features[jnp.clip(offsets, 0, local_rows - 1)], 0.0)
    pivot_feats = lax.psum(picked, ("blk", "row"))
    pivot_norms = jnp.sum(pivot_feats * pivot_feats, axis=1)
    cross = amplitude * kernel_tile(features, own_norms, pivot_feats, pivot_norms)
    gram_part = lax.dot_general(
        cross,
        cross,
        (((0,), (0,)), ((), ())),
        precision=highest,
        preferred_element_type=jnp.float32,
    )
    projected_part = lax.dot_general(
        cross,
        product,
        (((0,), (0,)), ((), ())),
        precision=highest,
        preferred_element_type=jnp.float32,
    )
    gram_sum, projected = lax.psum((gram_part, projected_part), ("blk", "row"))
    inner_pivots = amplitude * kernel_tile(pivot_feats, pivot_norms, pivot_feats, pivot_norms)
    gram = nugget * inner_pivots + gram_sum
    factor = jnp.linalg.cholesky(gram)
    coefficients = jax.scipy.linalg.cho_solve((factor, True), projected)
    preconditioned = (
        product
        - jnp.dot(cross, coefficients, precision=highest, preferred_element_type=jnp.float32)
    ) / nugget
    return (product, preconditioned)


def solution(mesh):
    in_specs = (P(("blk", "row"), None), P(("blk", "row"), None), P(), P(), P())
    out_specs = (P(("blk", "row"), None), P(("blk", "row"), None))
    return jax.shard_map(
        per_device, mesh=mesh, in_specs=in_specs, out_specs=out_specs, check_vma=False
    )
```

profile of v0, /device:TPU:0, one launch (start us, length us, event | category | flops | bytes accessed | tf_op | source)
XLA Modules:
  0.0 363.2 jit_solution(4064739874456005614)
XLA Ops:
  8.0 5.5 %collective-permute-start = (f32[64,256]{1,0:T(8,128)}, f32[64,256]{1,0:T(8,128)S(1)}, u32[]{:S(2)}, u32[]{:S(2)}) collective-permute-start(f32[64,256]{1,0:T(8,128)} %param.5), channel_id=1, source_target_pairs={{2,0},{4,2},{6,4},{8,6},{10,8},{12,10},{14,12},{16,14},{18,16},{20... | collective-permute-start | bytes 196616 | tf_op jit(solution)/shard_map/ppermute | solution.py:16
  20.2 5.1 %all_gather.36 = f32[128,256]{1,0:T(8,128)S(1)} all-gather(f32[64,256]{1,0:T(8,128)S(1)} %copy-done), channel_id=1, replica_groups=mesh['blk'=16,'row'=2] {'row'}, dimensions={0}, use_global_device_ids=true | all-gather | bytes 196608 | tf_op jit(solution)/shard_map/all_gather | solution.py:68
  25.2 4.6 %all_gather.37 = f32[128,128]{1,0:T(8,128)S(1)} all-gather(f32[64,128]{1,0:T(8,128)S(1)} %copy-done.1), channel_id=1, replica_groups=mesh['blk'=16,'row'=2] {'row'}, dimensions={0}, use_global_device_ids=true | all-gather | bytes 98304 | tf_op jit(solution)/shard_map/all_gather | solution.py:69
  32.5 4.6 %all_gather.47 = f32[128,128]{1,0:T(8,128)S(1)} all-gather(f32[64,128]{1,0:T(8,128)S(1)} %collective-permute-done.9), channel_id=1, replica_groups=mesh['blk'=16,'row'=2] {'row'}, dimensions={0}, use_global_device_ids=true | all-gather | bytes 98304 | tf_op jit(solution)/shard_map/all_gather | solution.py:69
  37.1 3.2 collective-permute-start.7
  40.3 4.6 %all_gather.39 = f32[128,128]{1,0:T(8,128)S(1)} all-gather(f32[64,128]{1,0:T(8,128)S(1)} %collective-permute-done.1), channel_id=1, replica_groups=mesh['blk'=16,'row'=2] {'row'}, dimensions={0}, use_global_device_ids=true | all-gather | bytes 98304 | tf_op jit(solution)/shard_map/all_gather | solution.py:69
  46.3 4.6 %all_gather.43 = f32[128,128]{1,0:T(8,128)S(1)} all-gather(f32[64,128]{1,0:T(8,128)S(1)} %collective-permute-done.5), channel_id=1, replica_groups=mesh['blk'=16,'row'=2] {'row'}, dimensions={0}, use_global_device_ids=true | all-gather | bytes 98304 | tf_op jit(solution)/shard_map/all_gather | solution.py:69
  51.0 4.6 %all_gather.45 = f32[128,128]{1,0:T(8,128)S(1)} all-gather(f32[64,128]{1,0:T(8,128)S(1)} %collective-permute-done.7), channel_id=1, replica_groups=mesh['blk'=16,'row'=2] {'row'}, dimensions={0}, use_global_device_ids=true | all-gather | bytes 98304 | tf_op jit(solution)/shard_map/all_gather | solution.py:69
  55.5 3.0 collective-permute-start.8
  58.5 4.6 %all_gather.41 = f32[128,128]{1,0:T(8,128)S(1)} all-gather(f32[64,128]{1,0:T(8,128)S(1)} %collective-permute-done.3), channel_id=1, replica_groups=mesh['blk'=16,'row'=2] {'row'}, dimensions={0}, use_global_device_ids=true | all-gather | bytes 98304 | tf_op jit(solution)/shard_map/all_gather | solution.py:69
  63.1 4.9 %all_gather.38 = f32[128,256]{1,0:T(8,128)S(1)} all-gather(f32[64,256]{1,0:T(8,128)S(1)} %collective-permute-done), channel_id=1, replica_groups=mesh['blk'=16,'row'=2] {'row'}, dimensions={0}, use_global_device_ids=true | all-gather | bytes 196608 | tf_op jit(solution)/shard_map/all_gather | solution.py:68
  68.4 5.0 %all_gather.40 = f32[128,256]{1,0:T(8,128)S(1)} all-gather(f32[64,256]{1,0:T(8,128)S(1)} %collective-permute-done.2), channel_id=1, replica_groups=mesh['blk'=16,'row'=2] {'row'}, dimensions={0}, use_global_device_ids=true | all-gather | bytes 196608 | tf_op jit(solution)/shard_map/all_gather | solution.py:68
  73.9 5.6 %all_gather.42 = f32[128,256]{1,0:T(8,128)S(1)} all-gather(f32[64,256]{1,0:T(8,128)S(1)} %collective-permute-done.4), channel_id=1, replica_groups=mesh['blk'=16,'row'=2] {'row'}, dimensions={0}, use_global_device_ids=true | all-gather | bytes 196608 | tf_op jit(solution)/shard_map/all_gather | solution.py:68
  79.9 4.9 %all_gather.46 = f32[128,256]{1,0:T(8,128)S(1)} all-gather(f32[64,256]{1,0:T(8,128)S(1)} %collective-permute-done.8), channel_id=1, replica_groups=mesh['blk'=16,'row'=2] {'row'}, dimensions={0}, use_global_device_ids=true | all-gather | bytes 196608 | tf_op jit(solution)/shard_map/all_gather | solution.py:68
  85.2 4.9 %all_gather.44 = f32[128,256]{1,0:T(8,128)S(1)} all-gather(f32[64,256]{1,0:T(8,128)S(1)} %collective-permute-done.6), channel_id=1, replica_groups=mesh['blk'=16,'row'=2] {'row'}, dimensions={0}, use_global_device_ids=true | all-gather | bytes 196608 | tf_op jit(solution)/shard_map/all_gather | solution.py:68
  95.3 52.4 %all-reduce.5.cloned.1.call-done = f32[256,256]{0,1:T(8,128)} async-done(((f32[256,256]{0,1:T(8,128)}), f32[256,256]{0,1:T(8,128)}) %all-reduce.5.cloned.1.call-update) | async-done | bytes 262160 | tf_op jit(solution)/shard_map/psum | solution.py:123
  152.9 2.4 collective-permute-start.12
  155.9 2.4 collective-permute-start.14
  162.4 128.9 %all-reduce.7.cloned.1.call-done = (f32[256,128]{1,0:T(8,128)}, f32[256,256]{0,1:T(8,128)}) async-done(((f32[256,128]{1,0:T(8,128)}, f32[256,256]{0,1:T(8,128)}), (f32[256,128]{1,0:T(8,128)}, f32[256,256]{0,1:T(8,128)})) %all-reduce.7.cloned.1.call-update) | async-done | bytes 393232 | tf_op jit(solution)/shard_map/psum | solution.py:140
  293.2 11.7 %cholesky.49 = f32[128,128]{1,0:T(8,128)S(1)} custom-call(f32[128,128]{1,0:T(8,128)S(1)} %cholesky.115), custom_call_target="Cholesky" | custom-call | tf_op jit(solution)/shard_map/jit(cholesky)/cholesky | solution.py:143
  304.9 9.8 %custom-call.18 = f32[1,128,128]{1,2,0:T(8,128)S(1)} custom-call(f32[1,128,128]{2,1,0:T(8,128)S(1)} %get-tuple-element.29), custom_call_target="InvertDiagBlocksLowerTriangular" | custom-call | tf_op jit(solution)/shard_map/jit(cholesky)/cholesky | solution.py:143
  315.2 11.7 %cholesky.103 = f32[128,128]{1,0:T(8,128)S(1)} custom-call(f32[128,128]{1,0:T(8,128)S(1)} %convolution_subtract_fusion.2), custom_call_target="Cholesky" | custom-call | tf_op jit(solution)/shard_map/jit(cholesky)/cholesky | solution.py:143
  329.4 4.4 %while.1 = (s32[]{:T(128)}, f32[256,256]{0,1:T(8,128)S(1)}, s32[2,2]{1,0:T(2,128)S(1)}, f32[2,128,128]{2,1,0:T(8,128)S(1)}, s32[]{:T(128)}) while((s32[]{:T(128)}, f32[256,256]{0,1:T(8,128)S(1)}, s32[2,2]{1,0:T(2,128)S(1)}, f32[2,128,128]{2,1,0:T(8,128)S(1)}, s32[]{:T(128)}) %tuple.27), condition=%wide.while_cond, body=%wide.while_body.sunk | while | flops 2 | bytes 393321 | solution.py:144
  333.7 19.7 %custom-call.19 = f32[2,128,128]{1,2,0:T(8,128)S(1)} custom-call(f32[2,128,128]{2,1,0:T(8,128)S(1)} %get-tuple-element.9), custom_call_target="InvertDiagBlocksLowerTriangular" | custom-call | tf_op jit(solution)/shard_map/jit(_cho_solve)/triangular_solve | solution.py:144
  (131 shorter events, 35.7 us)
Async XLA Ops:
  8.0 139.7 %all-reduce.5.cloned.1.call-start = ((), (), s32[]{:S(2)}) async-start(), calls=%async_computation.2 | async-start | bytes 524288 | tf_op jit(solution)/shard_map/psum | solution.py:123
  8.0 55.0 %collective-permute-start = (f32[64,256]{1,0:T(8,128)}, f32[64,256]{1,0:T(8,128)S(1)}, u32[]{:S(2)}, u32[]{:S(2)}) collective-permute-start(f32[64,256]{1,0:T(8,128)} %param.5), channel_id=1, source_target_pairs={{2,0},{4,2},{6,4},{8,6},{10,8},{12,10},{14,12},{16,14},{18,16},{20... | collective-permute-start | bytes 196616 | tf_op jit(solution)/shard_map/ppermute | solution.py:16
  13.6 54.8 %collective-permute-start.2 = (f32[64,256]{1,0:T(8,128)}, f32[64,256]{1,0:T(8,128)S(1)}, u32[]{:S(2)}, u32[]{:S(2)}) collective-permute-start(f32[64,256]{1,0:T(8,128)} %param.5), channel_id=1, source_target_pairs={{4,0},{6,2},{8,4},{10,6},{12,8},{14,10},{16,12},{18,14},{20,16},{2... | collective-permute-start | bytes 196616 | tf_op jit(solution)/shard_map/ppermute | solution.py:16
  14.2 59.7 %collective-permute-start.4 = (f32[64,256]{1,0:T(8,128)}, f32[64,256]{1,0:T(8,128)S(1)}, u32[]{:S(2)}, u32[]{:S(2)}) collective-permute-start(f32[64,256]{1,0:T(8,128)} %param.5), channel_id=1, source_target_pairs={{6,0},{8,2},{10,4},{12,6},{14,8},{16,10},{18,12},{20,14},{22,16},{... | collective-permute-start | bytes 196616 | tf_op jit(solution)/shard_map/ppermute | solution.py:16
  14.4 22.7 %collective-permute-start.1 = (f32[64,128]{1,0:T(8,128)}, f32[64,128]{1,0:T(8,128)S(1)}, u32[]{:S(2)}, u32[]{:S(2)}) collective-permute-start(f32[64,128]{1,0:T(8,128)} %param.6), channel_id=1, source_target_pairs={{2,0},{4,2},{6,4},{8,6},{10,8},{12,10},{14,12},{16,14},{18,16},{20... | collective-permute-start | bytes 98312 | tf_op jit(solution)/shard_map/ppermute | solution.py:16
  15.8 15.9 %collective-permute-start.9 = (f32[64,128]{1,0:T(8,128)}, f32[64,128]{1,0:T(8,128)S(1)}, u32[]{:S(2)}, u32[]{:S(2)}) collective-permute-start(f32[64,128]{1,0:T(8,128)} %param.6), channel_id=1, source_target_pairs={{16,0},{18,2},{20,4},{22,6},{24,8},{26,10},{28,12},{30,14},{0,16},... | collective-permute-start | bytes 98312 | tf_op jit(solution)/shard_map/ppermute | solution.py:16
  19.2 0.8 copy-start
  19.2 129.9 %reduce-scatter.2.cloned.1.call-start = ((), (), s32[]{:S(2)}) async-start(), calls=%async_computation.1 | async-start | bytes 589824 | tf_op jit(solution)/shard_map/reduce_scatter | solution.py:113
  20.2 5.1 %copy-start.1 = (f32[64,128]{1,0:T(8,128)S(1)}, f32[64,128]{1,0:T(8,128)}, u32[]{:S(2)}) copy-start(f32[64,128]{1,0:T(8,128)} %param.6) | copy-start | bytes 98308
  31.7 13.2 %collective-permute-start.5 = (f32[64,128]{1,0:T(8,128)S(1)}, f32[64,128]{1,0:T(8,128)S(1)}, u32[]{:S(2)}, u32[]{:S(2)}) collective-permute-start(f32[64,128]{1,0:T(8,128)S(1)} %copy-done.1), channel_id=1, source_target_pairs={{6,0},{8,2},{10,4},{12,6},{14,8},{16,10},{18,12},{20,14},{22,16},{... | collective-permute-start | bytes 98312 | tf_op jit(solution)/shard_map/ppermute | solution.py:16
  37.1 13.8 %collective-permute-start.7 = (f32[64,128]{1,0:T(8,128)S(1)}, f32[64,128]{1,0:T(8,128)S(1)}, u32[]{:S(2)}, u32[]{:S(2)}) collective-permute-start(f32[64,128]{1,0:T(8,128)S(1)} %copy-done.1), channel_id=1, source_target_pairs={{8,0},{10,2},{12,4},{14,6},{16,8},{18,10},{20,12},{22,14},{24,16},... | collective-permute-start | bytes 98312 | tf_op jit(solution)/shard_map/ppermute | solution.py:16
  44.9 10.7 %collective-permute-start.3 = (f32[64,128]{1,0:T(8,128)S(1)}, f32[64,128]{1,0:T(8,128)S(1)}, u32[]{:S(2)}, u32[]{:S(2)}) collective-permute-start(f32[64,128]{1,0:T(8,128)S(1)} %copy-done.1), channel_id=1, source_target_pairs={{4,0},{6,2},{8,4},{10,6},{12,8},{14,10},{16,12},{18,14},{20,16},{2... | collective-permute-start | bytes 98312 | tf_op jit(solution)/shard_map/ppermute | solution.py:16
  50.9 34.3 %collective-permute-start.6 = (f32[64,256]{1,0:T(8,128)S(1)}, f32[64,256]{1,0:T(8,128)S(1)}, u32[]{:S(2)}, u32[]{:S(2)}) collective-permute-start(f32[64,256]{1,0:T(8,128)S(1)} %copy-done), channel_id=1, source_target_pairs={{8,0},{10,2},{12,4},{14,6},{16,8},{18,10},{20,12},{22,14},{24,16},... | collective-permute-start | bytes 196616 | tf_op jit(solution)/shard_map/ppermute | solution.py:16
  55.5 24.4 %collective-permute-start.8 = (f32[64,256]{1,0:T(8,128)S(1)}, f32[64,256]{1,0:T(8,128)S(1)}, u32[]{:S(2)}, u32[]{:S(2)}) collective-permute-start(f32[64,256]{1,0:T(8,128)S(1)} %copy-done), channel_id=1, source_target_pairs={{16,0},{18,2},{20,4},{22,6},{24,8},{26,10},{28,12},{30,14},{0,16},... | collective-permute-start | bytes 196616 | tf_op jit(solution)/shard_map/ppermute | solution.py:16
  94.6 196.6 %all-reduce.7.cloned.1.call-start = ((), (), s32[]{:S(2)}) async-start(), calls=%async_computation.3 | async-start | bytes 786432 | tf_op jit(solution)/shard_map/psum | solution.py:140
  147.7 1.1 copy-start.2
  149.1 3.6 copy-start.5
  150.2 9.2 %collective-permute-start.10 = (f32[64,128]{1,0:T(8,128)S(1)}, f32[64,128]{1,0:T(8,128)S(1)}, u32[]{:S(2)}, u32[]{:S(2)}) collective-permute-start(f32[64,128]{1,0:T(8,128)S(1)} %convolution_add_fusion.3), channel_id=1, source_target_pairs={{30,0},{0,2},{2,4},{4,6},{6,8},{8,10},{10,12},{12,14},{14,16},{16,... | collective-permute-start | bytes 98312 | tf_op jit(solution)/shard_map/ppermute | solution.py:16
  151.2 8.2 %collective-permute-start.11 = (f32[64,128]{1,0:T(8,128)S(1)}, f32[64,128]{1,0:T(8,128)S(1)}, u32[]{:S(2)}, u32[]{:S(2)}) collective-permute-start(f32[64,128]{1,0:T(8,128)S(1)} %convolution_add_fusion.2), channel_id=1, source_target_pairs={{28,0},{30,2},{0,4},{2,6},{4,8},{6,10},{8,12},{10,14},{12,16},{14,... | collective-permute-start | bytes 98312 | tf_op jit(solution)/shard_map/ppermute | solution.py:16
  152.9 6.5 %collective-permute-start.12 = (f32[64,128]{1,0:T(8,128)S(1)}, f32[64,128]{1,0:T(8,128)S(1)}, u32[]{:S(2)}, u32[]{:S(2)}) collective-permute-start(f32[64,128]{1,0:T(8,128)S(1)} %convolution_add_fusion.1), channel_id=1, source_target_pairs={{26,0},{28,2},{30,4},{0,6},{2,8},{4,10},{6,12},{8,14},{10,16},{12,... | collective-permute-start | bytes 98312 | tf_op jit(solution)/shard_map/ppermute | solution.py:16
  155.3 5.7 %collective-permute-start.13 = (f32[64,128]{1,0:T(8,128)S(1)}, f32[64,128]{1,0:T(8,128)S(1)}, u32[]{:S(2)}, u32[]{:S(2)}) collective-permute-start(f32[64,128]{1,0:T(8,128)S(1)} %get-tuple-element.26), channel_id=1, source_target_pairs={{24,0},{26,2},{28,4},{30,6},{0,8},{2,10},{4,12},{6,14},{8,16},{10,... | collective-permute-start | bytes 98312 | tf_op jit(solution)/shard_map/ppermute | solution.py:16
  155.9 5.2 %collective-permute-start.14 = (f32[64,128]{1,0:T(8,128)S(1)}, f32[64,128]{1,0:T(8,128)S(1)}, u32[]{:S(2)}, u32[]{:S(2)}) collective-permute-start(f32[64,128]{1,0:T(8,128)S(1)} %get-tuple-element.27), channel_id=1, source_target_pairs={{16,0},{18,2},{20,4},{22,6},{24,8},{26,10},{28,12},{30,14},{0,16},... | collective-permute-start | bytes 98312 | tf_op jit(solution)/shard_map/ppermute | solution.py:16
  161.3 193.7 %copy-start.4 = (f32[64,128]{1,0:T(8,128)}, f32[64,128]{1,0:T(8,128)S(1)}, u32[]{:S(2)}) copy-start(f32[64,128]{1,0:T(8,128)S(1)} %fusion.31) | copy-start | bytes 98308
  329.4 24.0 %copy-start.6 = (f32[256,128]{1,0:T(8,128)S(1)}, f32[256,128]{1,0:T(8,128)}, u32[]{:S(2)}) copy-start(f32[256,128]{1,0:T(8,128)} %get-tuple-element.22) | copy-start | bytes 393220
  (2 other events, 1.4 us)
Sparse Core Ops, SparseCore 0:
  19.4 128.3 all-reduce.4
  162.5 128.7 all-reduce.6
Sparse Core Ops, SparseCore 1:
  94.7 10.7 reduce-scatter.1
where the time goes:
time: 364 us; the launch traced here: 363 us
  waiting for transfers between devices  183 us (50%)
  blocking collectives  57.9 us (16%)
  other arithmetic  56.6 us (16%)
  starting transfers between devices  23.3 us (6%)
  between operations  18.6 us (5%)
  matrix products  14.9 us (4%)
  local copies, waits for them, and re-layouts  8.57 us (2%)
    psum x1, waiting for transfers between devices, per_device(): gram_sum, projected = lax.psum((gram_part, projected_part), ('blk', 'row'))  129 us
    psum x1, waiting for transfers between devices, per_device(): pivot_feats = lax.psum(picked, ('blk', 'row'))  52.4 us
    another operation x6, other arithmetic, per_device(): factor = jnp.linalg.cholesky(gram)  34 us
    all_gather x6, blocking collectives, member_sweep(): arrived_feats = lax.all_gather(fetched[upper][0], 'row', axis=0, tiled=True)  30.5 us
    all_gather x6, blocking collectives, member_sweep(): lax.all_gather(fetched[upper][1], 'row', axis=0, tiled=True)  27.4 us
    ppermute x15, starting transfers between devices, shifted(): return lax.ppermute(block, axis, route)  23.2 us
    another operation x3, other arithmetic, per_device(): coefficients = jax.scipy.linalg.cho_solve((factor, True), projected)  19.7 us
  transfers between devices with their start and end apart: 18, of which 3 were waited for; matrix products, arithmetic and copies ran while one was open for 4% of the time, Pallas kernels for 0%

commit v1 on v0

v1 whole, which is shorter than its diff:
```python
import functools

import jax
import jax.numpy as jnp
from jax import lax
from jax.experimental import pallas as pl
from jax.experimental.pallas import tpu as pltpu
from jax.sharding import PartitionSpec as P

highest = lax.Precision.HIGHEST
root_five = 2.23606797749979
tiny = 1e-30
AXES = ("blk", "row")
NT = (((1,), (1,)), ((), ()))
NN = (((1,), (0,)), ((), ()))


def split(value):
    high = value.astype(jnp.bfloat16)
    low = (value - high.astype(jnp.float32)).astype(jnp.bfloat16)
    return high, low


def dot3(left, right, dims):
    left_high, left_low = left
    right_high, right_low = right
    product = functools.partial(
        lax.dot_general, dimension_numbers=dims, preferred_element_type=jnp.float32
    )
    return (
        product(left_high, right_low) + product(left_low, right_high) + product(left_high, right_high)
    )


def dot6(left, right, dims):
    return lax.dot_general(left, right, dims, precision=highest, preferred_element_type=jnp.float32)


def matern(row_feats, row_norms, col_feats, col_norms):
    five_squared = dot6(row_feats, col_feats, NT) + row_norms + col_norms
    five_squared = jnp.maximum(five_squared, tiny)
    scaled = five_squared * lax.rsqrt(five_squared)
    return (1.0 + scaled + five_squared * (1.0 / 3.0)) * jnp.exp(-scaled)


def lane_norms(feats):
    ones = jnp.full((8, feats.shape[1]), 5.0, jnp.float32)
    return dot6(ones, feats * feats, NT)[0:1, :]


def tile_kernel(index_ref, scalar_ref, *refs):
    pieces = refs[:8]
    probes_ref, gram_ref, send_ref, keep_ref, cross_ref, all_ref, query_ref = refs[8:]
    line_rows, feature_count = pieces[0].shape
    rank = gram_ref.shape[0]
    local_rows = cross_ref.shape[0]
    amplitude = scalar_ref[0]
    nugget = scalar_ref[1]
    for position, piece in enumerate(pieces):
        all_ref[position * line_rows : (position + 1) * line_rows, :] = piece[:, :]

    def pick(step, carry):
        query_ref[pl.ds(step, 1), :] = all_ref[pl.ds(index_ref[step], 1), :]
        return carry

    lax.fori_loop(0, rank, pick, 0, unroll=8)
    pivot_feats = query_ref[:rank, :]
    line_feats = pieces[0][:, :]
    query_ref[rank:, :] = line_feats
    query = query_ref[:, :]
    query_norms = 5.0 * jnp.sum(query * query, axis=1, keepdims=True)
    query_scaled = -10.0 * query
    pivot_norms = lane_norms(pivot_feats)
    line_norms = lane_norms(line_feats)
    probes = split(probes_ref[:, :])
    total = None
    line_cross = None
    for position, piece in enumerate(pieces):
        feats = piece[:, :]
        tile = matern(query_scaled, query_norms, feats, lane_norms(feats))
        halves = split(tile)
        part = dot3((halves[0][:rank], halves[1][:rank]), halves, NT)
        total = part if total is None else total + part
        if position == 0:
            line_cross = tile[:rank, :]
        own = feats[:local_rows, :]
        own_norms = 5.0 * jnp.sum(own * own, axis=1, keepdims=True)
        own_tile = matern(-10.0 * own, own_norms, line_feats, line_norms)
        rows = dot3(split(own_tile), probes, NN)
        if position < 4:
            keep_ref[position * local_rows : (position + 1) * local_rows, :] = rows
        else:
            send_ref[(position - 4) * local_rows : (position - 3) * local_rows, :] = rows
        if position == 0:
            cross_ref[:, :] = amplitude * matern(-10.0 * own, own_norms, pivot_feats, pivot_norms)
    inner = matern(query_scaled[:rank], query_norms[:rank], pivot_feats, pivot_norms)
    square = amplitude * amplitude
    gram_ref[:, :] = (nugget * amplitude) * inner + square * total[:, :rank]
    mixed = square * total[:, rank:] + (nugget * amplitude) * line_cross
    projected = dot3(split(mixed), probes, NN)
    keep_ref[4 * local_rows :, :] = projected
    send_ref[4 * local_rows :, :] = projected


def exchanged(value, mask, count):
    return lax.ppermute(value, AXES, [(i, i ^ mask) for i in range(count)])


def small_slice(features, probes, outputscale, noise, pivots):
    local_rows, probe_count = probes.shape
    feature_count = features.shape[1]
    rank = pivots.shape[0]
    row_count = lax.axis_size("row")
    count = lax.axis_size("blk") * row_count
    flat_index = lax.axis_index("blk") * row_count + lax.axis_index("row")
    step_x, step_core, step_y, step_z = 1, row_count, 2 * row_count, 4 * row_count
    send = functools.partial(exchanged, count=count)

    owner = (pivots // local_rows) ^ flat_index
    slot = (owner & 1) + 2 * ((owner // step_y) & 1) + 4 * ((owner // step_core) & 1)
    index = (slot * 4 + owner // step_z) * local_rows + pivots % local_rows

    packed = jnp.concatenate([features, probes], axis=1)
    line = [packed] + [send(packed, step_z * step) for step in (1, 2, 3)]
    line_feats = jnp.concatenate([part[:, :feature_count] for part in line], axis=0)
    line_probes = jnp.concatenate([part[:, feature_count:] for part in line], axis=0)
    pieces = [line_feats] + [send(line_feats, mask) for mask in (step_x, step_y, step_x + step_y)]
    pieces = pieces + [send(piece, step_core) for piece in pieces]

    vmem = pl.BlockSpec(memory_space=pltpu.VMEM)
    smem = pl.BlockSpec(memory_space=pltpu.SMEM)
    half = 4 * local_rows + rank
    gram, outgoing, kept, cross = pl.pallas_call(
        tile_kernel,
        out_shape=(
            jax.ShapeDtypeStruct((rank, rank), jnp.float32),
            jax.ShapeDtypeStruct((half, probe_count), jnp.float32),
            jax.ShapeDtypeStruct((half, probe_count), jnp.float32),
            jax.ShapeDtypeStruct((local_rows, rank), jnp.float32),
        ),
        in_specs=[smem, smem] + [vmem] * 9,
        out_specs=(vmem,) * 4,
        scratch_shapes=[
            pltpu.VMEM((8 * 4 * local_rows, feature_count), jnp.float32),
            pltpu.VMEM((rank + 4 * local_rows, feature_count), jnp.float32),
        ],
        name="tiles",
    )(index, jnp.concatenate([outputscale, noise]), *pieces, line_probes)

    amplitude = outputscale[0]
    nugget = noise[0]
    kept = kept + send(outgoing, step_core)
    part = lambda position: kept[position * local_rows : (position + 1) * local_rows]
    projected = kept[4 * local_rows :]
    arrived = send(jnp.concatenate([part(1), part(3), projected]), step_x)
    first = part(0) + arrived[:local_rows]
    third = part(2) + arrived[local_rows : 2 * local_rows]
    projected = projected + arrived[2 * local_rows :]
    arrived = send(jnp.concatenate([third, projected]), step_y)
    product = amplitude * (first + arrived[:local_rows]) + nugget * probes
    projected = projected + arrived[local_rows:]
    factor = jnp.linalg.cholesky(gram)
    coefficients = jax.scipy.linalg.cho_solve((factor, True), projected)
    correction = jnp.dot(cross, coefficients, precision=highest, preferred_element_type=jnp.float32)
    return product, (product - correction) / nugget


def plain_tile(row_feats, col_feats):
    row_norms = 5.0 * jnp.sum(row_feats * row_feats, axis=1)[:, None]
    col_norms = 5.0 * jnp.sum(col_feats * col_feats, axis=1)[None, :]
    return matern(-10.0 * row_feats, row_norms, col_feats, col_norms)


def large_slice(features, probes, outputscale, noise, pivots):
    dot = functools.partial(jnp.dot, precision=highest, preferred_element_type=jnp.float32)
    amplitude = outputscale[0]
    nugget = noise[0]
    all_feats = lax.all_gather(features, AXES, axis=0, tiled=True)
    all_probes = lax.all_gather(probes, AXES, axis=0, tiled=True)
    product = amplitude * dot(plain_tile(features, all_feats), all_probes) + nugget * probes
    pivot_feats = all_feats[pivots]
    cross = amplitude * plain_tile(features, pivot_feats)
    inner = amplitude * plain_tile(pivot_feats, pivot_feats)
    gram, projected = lax.psum((dot(cross.T, cross), dot(cross.T, product)), AXES)
    factor = jnp.linalg.cholesky(nugget * inner + gram)
    coefficients = jax.scipy.linalg.cho_solve((factor, True), projected)
    return product, (product - dot(cross, coefficients)) / nugget


def solution(mesh):
    small = mesh.shape["blk"] == 16 and mesh.shape["row"] == 2
    in_specs = (P(AXES, None), P(AXES, None), P(), P(), P())
    out_specs = (P(AXES, None), P(AXES, None))
    return jax.shard_map(
        small_slice if small else large_slice,
        mesh=mesh,
        in_specs=in_specs,
        out_specs=out_specs,
        check_vma=False,
    )
```

time: 364 us -> 127 us (0.35)
  waiting for transfers between devices: 183 us -> 22.1 us
  blocking collectives: 57.9 us -> 0 us
  Pallas kernels: 0 us -> 18.4 us
  between operations: 18.6 us -> 3.57 us
  matrix products: 14.9 us -> 2.78 us
  starting transfers between devices: 23.3 us -> 12.7 us
    psum x2 -> x0, waiting for transfers between devices: 181 us -> none  [the longest x1 129 us: per_device(): gram_sum, projected = lax.psum((gram_part, projected_part), ('blk', 'row'))]
    all_gather x12 -> x0, blocking collectives: 57.9 us -> none  [the longest x6 30.5 us: member_sweep(): arrived_feats = lax.all_gather(fetched[upper][0], 'row', axis=0, tiled=True)]
    ppermute x15 -> x13, waiting for transfers between devices: 1.72 us -> 22.1 us  [exchanged(): return lax.ppermute(value, AXES, [(i, i ^ mask) for i in range(count)])]
    pallas_call x0 -> x1, Pallas kernels: none -> 18.4 us  [small_slice(): pl.pallas_call(tile_kernel, out_shape=(jax.ShapeDtypeStruct((rank, rank),...]
    dot_general x30 -> x1, matrix products: 12.9 us -> 0.84 us  [small_slice(): jnp.dot(cross, coefficients, precision=highest, preferred_element_type=jn...]
    ppermute x15 -> x13, starting transfers between devices: 23.2 us -> 12.7 us  [exchanged(): return lax.ppermute(value, AXES, [(i, i ^ mask) for i in range(count)])]
  transfers between devices with their start and end apart: 18 -> 13, of which waited for: 3 -> 5; matrix products, arithmetic and copies ran while one was open for 4% -> 21% of each run, Pallas kernels for 0% -> 0%
where the time goes in v1:
time: 127 us; the launch traced here: 126 us
  other arithmetic  56.1 us (44%)
  waiting for transfers between devices  22.1 us (17%)
  Pallas kernels  18.4 us (14%)
  starting transfers between devices  12.7 us (10%)
  local copies, waits for them, and re-layouts  10.6 us (8%)
  between operations  3.57 us (3%)
  matrix products  2.78 us (2%)
    another operation x6, other arithmetic, small_slice(): factor = jnp.linalg.cholesky(gram)  34.1 us
    ppermute x13, waiting for transfers between devices, exchanged(): return lax.ppermute(value, AXES, [(i, i ^ mask) for i in range(count)])  22.1 us
    another operation x3, other arithmetic, small_slice(): coefficients = jax.scipy.linalg.cho_solve((factor, True), projected)  19.9 us
    pallas_call x1, Pallas kernels, small_slice(): pl.pallas_call(tile_kernel, out_shape=(jax.ShapeDtypeStruct((rank, rank),...  18.4 us
    ppermute x13, starting transfers between devices, exchanged(): return lax.ppermute(value, AXES, [(i, i ^ mask) for i in range(count)])  12.7 us
    unnamed x37, local copies, waits for them, and re-layouts  4.73 us
    another operation x6, local copies, waits for them, and re-layouts  3.8 us
  transfers between devices with their start and end apart: 13, of which 5 were waited for; matrix products, arithmetic and copies ran while one was open for 21% of the time, Pallas kernels for 0%

profile of v1, /device:TPU:0, one launch (start us, length us, event | category | flops | bytes accessed | tf_op | source)
XLA Modules:
  0.0 126.3 jit_solution(15499270910966160708)
XLA Ops:
  0.6 0.9 constant_dynamic-update-slice_fusion.1
  1.5 3.1 %collective-permute-start = (f32[64,384]{1,0:T(8,128)S(1)}, f32[64,384]{1,0:T(8,128)S(1)}, u32[]{:S(2)}, u32[]{:S(2)}) collective-permute-start(f32[64,384]{1,0:T(8,128)S(1)} %constant_dynamic-update-slice_fusion), channel_id=1, source_target_pairs={{0,8},{1,9},{2,10},{3,11},{4,12},{5,13},{6,14},{7,15},{8,0},{9,1},... | collective-permute-start | bytes 294920 | tf_op jit(solution)/shard_map/ppermute | solution.py:106
  4.6 2.6 %collective-permute-start.1 = (f32[64,384]{1,0:T(8,128)S(1)}, f32[64,384]{1,0:T(8,128)S(1)}, u32[]{:S(2)}, u32[]{:S(2)}) collective-permute-start(f32[64,384]{1,0:T(8,128)S(1)} %constant_dynamic-update-slice_fusion), channel_id=1, source_target_pairs={{0,16},{1,17},{2,18},{3,19},{4,20},{5,21},{6,22},{7,23},{8,24},{9,... | collective-permute-start | bytes 294920 | tf_op jit(solution)/shard_map/ppermute | solution.py:106
  7.4 7.6 %collective-permute-done.1 = f32[64,384]{1,0:T(8,128)S(1)} collective-permute-done((f32[64,384]{1,0:T(8,128)S(1)}, f32[64,384]{1,0:T(8,128)S(1)}, u32[]{:S(2)}, u32[]{:S(2)}) %collective-permute-start.1) | collective-permute-done | bytes 98336 | tf_op jit(solution)/shard_map/ppermute | solution.py:106
  15.1 0.8 copy-done.11
  16.0 1.6 %collective-permute-start.3 = (f32[256,256]{1,0:T(8,128)S(1)}, f32[256,256]{1,0:T(8,128)S(1)}, u32[]{:S(2)}, u32[]{:S(2)}) collective-permute-start(f32[256,256]{1,0:T(8,128)S(1)} %pad_maximum_fusion.refs_0_), channel_id=1, source_target_pairs={{0,1},{1,0},{2,3},{3,2},{4,5},{5,4},{6,7},{7,6},{8,9},{9,8},{10,11... | collective-permute-start | bytes 786440 | tf_op jit(solution)/shard_map/ppermute | solution.py:106
  17.6 1.5 %collective-permute-start.4 = (f32[256,256]{1,0:T(8,128)S(1)}, f32[256,256]{1,0:T(8,128)S(1)}, u32[]{:S(2)}, u32[]{:S(2)}) collective-permute-start(f32[256,256]{1,0:T(8,128)S(1)} %pad_maximum_fusion.refs_0_), channel_id=1, source_target_pairs={{0,4},{1,5},{2,6},{3,7},{4,0},{5,1},{6,2},{7,3},{8,12},{9,13},{10,... | collective-permute-start | bytes 786440 | tf_op jit(solution)/shard_map/ppermute | solution.py:106
  20.8 4.2 %collective-permute-done.3.refs_1_ = f32[256,256]{1,0:T(8,128)S(1)} collective-permute-done((f32[256,256]{1,0:T(8,128)S(1)}, f32[256,256]{1,0:T(8,128)S(1)}, u32[]{:S(2)}, u32[]{:S(2)}) %collective-permute-start.3) | collective-permute-done | bytes 262176 | tf_op jit(solution)/shard_map/ppermute | solution.py:106
  25.0 4.0 %collective-permute-done.4.refs_2_ = f32[256,256]{1,0:T(8,128)S(1)} collective-permute-done((f32[256,256]{1,0:T(8,128)S(1)}, f32[256,256]{1,0:T(8,128)S(1)}, u32[]{:S(2)}, u32[]{:S(2)}) %collective-permute-start.4) | collective-permute-done | bytes 262176 | tf_op jit(solution)/shard_map/ppermute | solution.py:106
  31.6 0.7 slice-done.1
  34.6 18.4 %tiles.1 = (f32[256,256]{1,0:T(8,128)}, f32[512,128]{1,0:T(8,128)}, f32[512,128]{1,0:T(8,128)}, f32[64,256]{1,0:T(8,128)}) custom-call(s32[256]{0:T(256)} %fusion.18.index_ref, f32[2]{0:T(128)} %pad_maximum_fusion.4.scalar_ref, f32[256,256]{1,0:T(8,128)} %copy-done, f32[256,256]{1,0:T(8,128)} %copy-done.3, f32[256,256]{1,0:T(8,128)} %copy-done.4, ...), custom_call_target="tpu_custom_call" | custom-call | tf_op jit(solution)/shard_map/tiles/pallas_call | solution.py:133
  53.0 1.1 copy.7
  54.2 11.9 %cholesky.50 = f32[128,128]{1,0:T(8,128)S(1)} custom-call(f32[128,128]{1,0:T(8,128)S(1)} %cholesky.118), custom_call_target="Cholesky" | custom-call | tf_op jit(solution)/shard_map/jit(cholesky)/cholesky | solution.py:162
  66.2 9.8 %custom-call.18 = f32[1,128,128]{1,2,0:T(8,128)S(1)} custom-call(f32[1,128,128]{2,1,0:T(8,128)S(1)} %get-tuple-element.31), custom_call_target="InvertDiagBlocksLowerTriangular" | custom-call | tf_op jit(solution)/shard_map/jit(cholesky)/cholesky | solution.py:162
  76.5 11.7 %cholesky.105 = f32[128,128]{1,0:T(8,128)S(1)} custom-call(f32[128,128]{1,0:T(8,128)S(1)} %slice_subtract_fusion.2), custom_call_target="Cholesky" | custom-call | tf_op jit(solution)/shard_map/jit(cholesky)/cholesky | solution.py:162
  90.4 1.2 collective-permute-start.11
  91.6 6.1 %collective-permute-done.11 = f32[384,128]{1,0:T(8,128)S(1)} collective-permute-done((f32[384,128]{1,0:T(8,128)S(1)}, f32[384,128]{1,0:T(8,128)S(1)}, u32[]{:S(2)}, u32[]{:S(2)}) %collective-permute-start.11) | collective-permute-done | bytes 196640 | tf_op jit(solution)/shard_map/ppermute | solution.py:106
  97.7 1.6 %collective-permute-start.12 = (f32[320,128]{1,0:T(8,128)S(1)}, f32[320,128]{1,0:T(8,128)S(1)}, u32[]{:S(2)}, u32[]{:S(2)}) collective-permute-start(f32[320,128]{1,0:T(8,128)S(1)} %pad_maximum_fusion.2), channel_id=1, source_target_pairs={{0,4},{1,5},{2,6},{3,7},{4,0},{5,1},{6,2},{7,3},{8,12},{9,13},{10,... | collective-permute-start | bytes 491528 | tf_op jit(solution)/shard_map/ppermute | solution.py:106
  99.4 3.8 %while.1 = (s32[]{:T(128)}, f32[256,256]{1,0:T(8,128)S(1)}, s32[2,2]{1,0:T(2,128)S(1)}, f32[2,128,128]{2,1,0:T(8,128)S(1)}, s32[]{:T(128)}) while((s32[]{:T(128)}, f32[256,256]{1,0:T(8,128)S(1)}, s32[2,2]{1,0:T(2,128)S(1)}, f32[2,128,128]{2,1,0:T(8,128)S(1)}, s32[]{:T(128)}) %tuple.27), condition=%wide.while_cond, body=%wide.while_body.sunk | while | flops 2 | bytes 131181 | solution.py:163
  100.0 1.3 %bitcast_dynamic-update-slice_fusion.2 = f32[2,128,128]{2,1,0:T(8,128)S(1)} fusion(f32[2,128,128]{2,1,0:T(8,128)S(1)} %get-tuple-element.73, s32[]{:T(128)} %get-tuple-element.70, f32[256,256]{1,0:T(8,128)S(1)} %get-tuple-element.76, s32[]{:T(128)} %bitcast.36, s32[]{:T(128)} %bitcast.37), kind=kLoop, calls=%fused_computation.clone.1 | loop fusion | bytes 131084 | tf_op jit(solution)/shard_map/jit(_cho_solve)/triangular_solve
  101.9 1.3 %bitcast_dynamic-update-slice_fusion.2 = f32[2,128,128]{2,1,0:T(8,128)S(1)} fusion(f32[2,128,128]{2,1,0:T(8,128)S(1)} %get-tuple-element.73, s32[]{:T(128)} %get-tuple-element.70, f32[256,256]{1,0:T(8,128)S(1)} %get-tuple-element.76, s32[]{:T(128)} %bitcast.36, s32[]{:T(128)} %bitcast.37), kind=kLoop, calls=%fused_computation.clone.1 | loop fusion | bytes 131084 | tf_op jit(solution)/shard_map/jit(_cho_solve)/triangular_solve
  103.2 19.9 %custom-call.19 = f32[2,128,128]{1,2,0:T(8,128)S(1)} custom-call(f32[2,128,128]{2,1,0:T(8,128)S(1)} %get-tuple-element.17), custom_call_target="InvertDiagBlocksLowerTriangular" | custom-call | tf_op jit(solution)/shard_map/jit(_cho_solve)/triangular_solve | solution.py:163
  124.7 0.8 copy-done.15
  125.5 0.8 fusion
  (94 shorter events, 9.8 us)
Async XLA Ops:
  1.5 5.9 %collective-permute-start = (f32[64,384]{1,0:T(8,128)S(1)}, f32[64,384]{1,0:T(8,128)S(1)}, u32[]{:S(2)}, u32[]{:S(2)}) collective-permute-start(f32[64,384]{1,0:T(8,128)S(1)} %constant_dynamic-update-slice_fusion), channel_id=1, source_target_pairs={{0,8},{1,9},{2,10},{3,11},{4,12},{5,13},{6,14},{7,15},{8,0},{9,1},... | collective-permute-start | bytes 294920 | tf_op jit(solution)/shard_map/ppermute | solution.py:106
  4.6 10.4 %collective-permute-start.1 = (f32[64,384]{1,0:T(8,128)S(1)}, f32[64,384]{1,0:T(8,128)S(1)}, u32[]{:S(2)}, u32[]{:S(2)}) collective-permute-start(f32[64,384]{1,0:T(8,128)S(1)} %constant_dynamic-update-slice_fusion), channel_id=1, source_target_pairs={{0,16},{1,17},{2,18},{3,19},{4,20},{5,21},{6,22},{7,23},{8,24},{9,... | collective-permute-start | bytes 294920 | tf_op jit(solution)/shard_map/ppermute | solution.py:106
  7.2 7.9 %collective-permute-start.2 = (f32[64,384]{1,0:T(8,128)S(1)}, f32[64,384]{1,0:T(8,128)S(1)}, u32[]{:S(2)}, u32[]{:S(2)}) collective-permute-start(f32[64,384]{1,0:T(8,128)S(1)} %constant_dynamic-update-slice_fusion), channel_id=1, source_target_pairs={{0,24},{1,25},{2,26},{3,27},{4,28},{5,29},{6,30},{7,31},{8,16},{9,... | collective-permute-start | bytes 294920 | tf_op jit(solution)/shard_map/ppermute | solution.py:106
  7.4 7.6 %copy-start.12 = (f32[64,384]{1,0:T(8,128)}, f32[64,384]{1,0:T(8,128)S(1)}, u32[]{:S(2)}) copy-start(f32[64,384]{1,0:T(8,128)S(1)} %collective-permute-done) | copy-start | bytes 294916
  15.0 16.5 %copy-start.14 = (f32[64,384]{1,0:T(8,128)}, f32[64,384]{1,0:T(8,128)S(1)}, u32[]{:S(2)}) copy-start(f32[64,384]{1,0:T(8,128)S(1)} %collective-permute-done.1) | copy-start | bytes 294916
  15.1 0.9 slice-start
  16.0 17.1 %copy-start = (f32[256,256]{1,0:T(8,128)}, f32[256,256]{1,0:T(8,128)S(1)}, u32[]{:S(2)}) copy-start(f32[256,256]{1,0:T(8,128)S(1)} %pad_maximum_fusion.refs_0_) | copy-start | bytes 786436
  16.0 9.0 %collective-permute-start.3 = (f32[256,256]{1,0:T(8,128)S(1)}, f32[256,256]{1,0:T(8,128)S(1)}, u32[]{:S(2)}, u32[]{:S(2)}) collective-permute-start(f32[256,256]{1,0:T(8,128)S(1)} %pad_maximum_fusion.refs_0_), channel_id=1, source_target_pairs={{0,1},{1,0},{2,3},{3,2},{4,5},{5,4},{6,7},{7,6},{8,9},{9,8},{10,11... | collective-permute-start | bytes 786440 | tf_op jit(solution)/shard_map/ppermute | solution.py:106
  17.6 11.5 %collective-permute-start.4 = (f32[256,256]{1,0:T(8,128)S(1)}, f32[256,256]{1,0:T(8,128)S(1)}, u32[]{:S(2)}, u32[]{:S(2)}) collective-permute-start(f32[256,256]{1,0:T(8,128)S(1)} %pad_maximum_fusion.refs_0_), channel_id=1, source_target_pairs={{0,4},{1,5},{2,6},{3,7},{4,0},{5,1},{6,2},{7,3},{8,12},{9,13},{10,... | collective-permute-start | bytes 786440 | tf_op jit(solution)/shard_map/ppermute | solution.py:106
  19.1 10.0 %collective-permute-start.5 = (f32[256,256]{1,0:T(8,128)S(1)}, f32[256,256]{1,0:T(8,128)S(1)}, u32[]{:S(2)}, u32[]{:S(2)}) collective-permute-start(f32[256,256]{1,0:T(8,128)S(1)} %pad_maximum_fusion.refs_0_), channel_id=1, source_target_pairs={{0,5},{1,4},{2,7},{3,6},{4,1},{5,0},{6,3},{7,2},{8,13},{9,12},{10,... | collective-permute-start | bytes 786440 | tf_op jit(solution)/shard_map/ppermute | solution.py:106
  20.8 12.2 %collective-permute-start.6 = (f32[256,256]{1,0:T(8,128)S(1)}, f32[256,256]{1,0:T(8,128)S(1)}, u32[]{:S(2)}, u32[]{:S(2)}) collective-permute-start(f32[256,256]{1,0:T(8,128)S(1)} %pad_maximum_fusion.refs_0_), channel_id=1, source_target_pairs={{0,2},{1,3},{2,0},{3,1},{4,6},{5,7},{6,4},{7,5},{8,10},{9,11},{10,... | collective-permute-start | bytes 786440 | tf_op jit(solution)/shard_map/ppermute | solution.py:106
  25.0 8.0 %copy-start.3 = (f32[256,256]{1,0:T(8,128)}, f32[256,256]{1,0:T(8,128)S(1)}, u32[]{:S(2)}) copy-start(f32[256,256]{1,0:T(8,128)S(1)} %collective-permute-done.3.refs_1_) | copy-start | bytes 786436
  25.0 8.0 %collective-permute-start.7 = (f32[256,256]{1,0:T(8,128)S(1)}, f32[256,256]{1,0:T(8,128)S(1)}, u32[]{:S(2)}, u32[]{:S(2)}) collective-permute-start(f32[256,256]{1,0:T(8,128)S(1)} %collective-permute-done.3.refs_1_), channel_id=1, source_target_pairs={{0,2},{1,3},{2,0},{3,1},{4,6},{5,7},{6,4},{7,5},{8,10},{9,11},{10,... | collective-permute-start | bytes 786440 | tf_op jit(solution)/shard_map/ppermute | solution.py:106
  29.1 4.0 %copy-start.4 = (f32[256,256]{1,0:T(8,128)}, f32[256,256]{1,0:T(8,128)S(1)}, u32[]{:S(2)}) copy-start(f32[256,256]{1,0:T(8,128)S(1)} %collective-permute-done.4.refs_2_) | copy-start | bytes 786436
  29.1 4.0 %collective-permute-start.8 = (f32[256,256]{1,0:T(8,128)S(1)}, f32[256,256]{1,0:T(8,128)S(1)}, u32[]{:S(2)}, u32[]{:S(2)}) collective-permute-start(f32[256,256]{1,0:T(8,128)S(1)} %collective-permute-done.4.refs_2_), channel_id=1, source_target_pairs={{0,2},{1,3},{2,0},{3,1},{4,6},{5,7},{6,4},{7,5},{8,10},{9,11},{10,... | collective-permute-start | bytes 786440 | tf_op jit(solution)/shard_map/ppermute | solution.py:106
  29.1 4.0 %copy-start.5 = (f32[256,256]{1,0:T(8,128)}, f32[256,256]{1,0:T(8,128)S(1)}, u32[]{:S(2)}) copy-start(f32[256,256]{1,0:T(8,128)S(1)} %collective-permute-done.5.refs_3_) | copy-start | bytes 786436
  29.1 4.0 %collective-permute-start.9 = (f32[256,256]{1,0:T(8,128)S(1)}, f32[256,256]{1,0:T(8,128)S(1)}, u32[]{:S(2)}, u32[]{:S(2)}) collective-permute-start(f32[256,256]{1,0:T(8,128)S(1)} %collective-permute-done.5.refs_3_), channel_id=1, source_target_pairs={{0,2},{1,3},{2,0},{3,1},{4,6},{5,7},{6,4},{7,5},{8,10},{9,11},{10,... | collective-permute-start | bytes 786440 | tf_op jit(solution)/shard_map/ppermute | solution.py:106
  53.0 1.2 copy-start.1
  76.0 12.2 %copy-start.17 = (f32[512,128]{1,0:T(8,128)S(1)}, f32[512,128]{1,0:T(8,128)}, u32[]{:S(2)}) copy-start(f32[512,128]{1,0:T(8,128)} %get-tuple-element.7) | copy-start | bytes 786436
  76.2 14.1 %copy-start.6 = (f32[512,128]{1,0:T(8,128)S(1)}, f32[512,128]{1,0:T(8,128)}, u32[]{:S(2)}) copy-start(f32[512,128]{1,0:T(8,128)} %get-tuple-element.6) | copy-start | bytes 786436
  88.2 2.1 %collective-permute-start.10 = (f32[512,128]{1,0:T(8,128)S(1)}, f32[512,128]{1,0:T(8,128)S(1)}, u32[]{:S(2)}, u32[]{:S(2)}) collective-permute-start(f32[512,128]{1,0:T(8,128)S(1)} %copy-done.17), channel_id=1, source_target_pairs={{0,2},{1,3},{2,0},{3,1},{4,6},{5,7},{6,4},{7,5},{8,10},{9,11},{10,... | collective-permute-start | bytes 786440 | tf_op jit(solution)/shard_map/ppermute | solution.py:106
  90.4 7.3 %collective-permute-start.11 = (f32[384,128]{1,0:T(8,128)S(1)}, f32[384,128]{1,0:T(8,128)S(1)}, u32[]{:S(2)}, u32[]{:S(2)}) collective-permute-start(f32[384,128]{1,0:T(8,128)S(1)} %pad_maximum_fusion.1), channel_id=1, source_target_pairs={{0,1},{1,0},{2,3},{3,2},{4,5},{5,4},{6,7},{7,6},{8,9},{9,8},{10,11... | collective-permute-start | bytes 589832 | tf_op jit(solution)/shard_map/ppermute | solution.py:106
  97.7 25.4 %collective-permute-start.12 = (f32[320,128]{1,0:T(8,128)S(1)}, f32[320,128]{1,0:T(8,128)S(1)}, u32[]{:S(2)}, u32[]{:S(2)}) collective-permute-start(f32[320,128]{1,0:T(8,128)S(1)} %pad_maximum_fusion.2), channel_id=1, source_target_pairs={{0,4},{1,5},{2,6},{3,7},{4,0},{5,1},{6,2},{7,3},{8,12},{9,13},{10,... | collective-permute-start | bytes 491528 | tf_op jit(solution)/shard_map/ppermute | solution.py:106
  124.7 1.6 %copy-start.13 = (f32[64,128]{1,0:T(8,128)}, f32[64,128]{1,0:T(8,128)S(1)}, u32[]{:S(2)}) copy-start(f32[64,128]{1,0:T(8,128)S(1)} %fusion.17) | copy-start | bytes 98308
  (10 other events, 7.9 us)

commit v2 on v1

--- a/solution.py
+++ b/solution.py
@@ -102,6 +102,97 @@
     send_ref[4 * local_rows :, :] = projected
 
 
+LANES, SUB, PANEL = 128, 8, 32
+
+def reciprocal(value):
+    guess = pl.reciprocal(value, approx=True)
+    return guess * (2.0 - value * guess)
+
+def panel_rows(matrix_ref, start):
+    tiles = matrix_ref.shape[1] // LANES
+    home = start // LANES
+    sublane = lax.broadcasted_iota(jnp.int32, (SUB, LANES), 0)
+    lane = lax.broadcasted_iota(jnp.int32, (SUB, LANES), 1)
+    groups = [
+        [matrix_ref[start + SUB * g : start + SUB * (g + 1), LANES * t : LANES * (t + 1)] for t in range(tiles)]
+        for g in range(PANEL // SUB)
+    ]
+    for own in range(PANEL // SUB):
+        base = (start + SUB * own) % LANES
+        columns = [
+            [jnp.broadcast_to(group[home][:, base + j : base + j + 1], (SUB, LANES)) for j in range(SUB)]
+            for group in groups
+        ]
+        rows = list(groups[own])
+        local = list(columns[own])
+        for j in range(SUB):
+            here = sublane == j
+            inverse = reciprocal(jnp.broadcast_to(local[j][j : j + 1, :], (SUB, LANES)))
+            factor = local[j]
+            for c in range(j + 1, SUB):
+                scaled = jnp.broadcast_to(local[c][j : j + 1, :], (SUB, LANES)) * inverse
+                local[c] = jnp.where(here, scaled, local[c] - factor * scaled)
+            unit = jnp.where(here, 1.0, 0.0)
+            rows[home] = jnp.where(lane == base + j, unit, rows[home])
+            for t in range(tiles):
+                scaled = jnp.broadcast_to(rows[t][j : j + 1, :], (SUB, LANES)) * inverse
+                rows[t] = jnp.where(here, scaled, rows[t] - factor * scaled)
+        groups[own] = rows
+        inside = (lane >= base) & (lane < base + SUB)
+        for g in range(PANEL // SUB):
+            if g != own:
+                for t in range(tiles):
+                    value = groups[g][t]
+                    if t == home:
+                        value = jnp.where(inside, 0.0, value)
+                    for j in range(SUB):
+                        value = value - columns[g][j] * jnp.broadcast_to(rows[t][j : j + 1, :], (SUB, LANES))
+                    groups[g][t] = value
+    return jnp.concatenate([jnp.concatenate(group, axis=1) for group in groups], axis=0)
+
+def eliminate(matrix_ref, start):
+    size = matrix_ref.shape[0]
+    home = start // LANES
+    solved = panel_rows(matrix_ref, start)
+    matrix_ref[start : start + PANEL, :] = solved
+    before = start % LANES
+    pad = [jnp.zeros((before, size), jnp.float32)] * (before > 0) + [solved] + [jnp.zeros((LANES - PANEL - before, size), jnp.float32)] * (before + PANEL < LANES)
+    padded = jnp.concatenate(pad, axis=0) if len(pad) > 1 else solved
+    after = start + PANEL
+    chunks = [(after, after + PANEL), (after + PANEL, size), (0, start)]
+    for low, high in chunks:
+        if low < high and low < size:
+            block = matrix_ref[low:high, LANES * home : LANES * (home + 1)]
+            update = dot6(block, padded, NN)
+            lane = lax.broadcasted_iota(jnp.int32, block.shape, 1)
+            inside = (lane >= before) & (lane < before + PANEL)
+            for t in range(size // LANES):
+                value = jnp.where(inside, 0.0, block) if t == home else matrix_ref[low:high, LANES * t : LANES * (t + 1)]
+                matrix_ref[low:high, LANES * t : LANES * (t + 1)] = value - update[:, LANES * t : LANES * (t + 1)]
+
+
+def invert_kernel(gram_ref, out_ref, *, first, last):
+    out_ref[:, :] = gram_ref[:, :]
+    for panel in range(first, last):
+        eliminate(out_ref, panel * PANEL)
+
+
+def weight_kernel(gram_ref, cross_ref, out_ref, work_ref, *, first, last):
+    invert_kernel(gram_ref, work_ref, first=first, last=last)
+    out_ref[:, :] = dot6(cross_ref[:, :], work_ref[:, :], NN)
+
+
+def final_kernel(scalar_ref, kept_ref, arrived_ref, probes_ref, weight_ref, product_ref, out_ref):
+    local_rows = probes_ref.shape[0]
+    nugget = scalar_ref[1]
+    kernel_probes = kept_ref[:local_rows, :] + arrived_ref[:local_rows, :]
+    projected = kept_ref[2 * local_rows :, :] + arrived_ref[local_rows:, :]
+    product = scalar_ref[0] * kernel_probes + nugget * probes_ref[:, :]
+    product_ref[:, :] = product
+    correction = dot6(weight_ref[:, :], projected, NN)
+    out_ref[:, :] = (product - correction) * (1.0 / nugget)
+
+
 def exchanged(value, mask, count):
     return lax.ppermute(value, AXES, [(i, i ^ mask) for i in range(count)])
 
@@ -117,16 +208,17 @@
     send = functools.partial(exchanged, count=count)
 
     owner = (pivots // local_rows) ^ flat_index
-    slot = (owner & 1) + 2 * ((owner // step_y) & 1) + 4 * ((owner // step_core) & 1)
+    slot = ((owner // step_y) & 1) + 2 * (owner & 1) + 4 * ((owner // step_core) & 1)
     index = (slot * 4 + owner // step_z) * local_rows + pivots % local_rows
 
     packed = jnp.concatenate([features, probes], axis=1)
     line = [packed] + [send(packed, step_z * step) for step in (1, 2, 3)]
     line_feats = jnp.concatenate([part[:, :feature_count] for part in line], axis=0)
     line_probes = jnp.concatenate([part[:, feature_count:] for part in line], axis=0)
-    pieces = [line_feats] + [send(line_feats, mask) for mask in (step_x, step_y, step_x + step_y)]
+    pieces = [line_feats] + [send(line_feats, mask) for mask in (step_y, step_x, step_x + step_y)]
     pieces = pieces + [send(piece, step_core) for piece in pieces]
 
+    scalars = jnp.concatenate([outputscale, noise])
     vmem = pl.BlockSpec(memory_space=pltpu.VMEM)
     smem = pl.BlockSpec(memory_space=pltpu.SMEM)
     half = 4 * local_rows + rank
@@ -145,24 +237,54 @@
             pltpu.VMEM((rank + 4 * local_rows, feature_count), jnp.float32),
         ],
         name="tiles",
-    )(index, jnp.concatenate([outputscale, noise]), *pieces, line_probes)
-
-    amplitude = outputscale[0]
-    nugget = noise[0]
-    kept = kept + send(outgoing, step_core)
-    part = lambda position: kept[position * local_rows : (position + 1) * local_rows]
-    projected = kept[4 * local_rows :]
-    arrived = send(jnp.concatenate([part(1), part(3), projected]), step_x)
-    first = part(0) + arrived[:local_rows]
-    third = part(2) + arrived[local_rows : 2 * local_rows]
-    projected = projected + arrived[2 * local_rows :]
-    arrived = send(jnp.concatenate([third, projected]), step_y)
-    product = amplitude * (first + arrived[:local_rows]) + nugget * probes
-    projected = projected + arrived[local_rows:]
-    factor = jnp.linalg.cholesky(gram)
-    coefficients = jax.scipy.linalg.cho_solve((factor, True), projected)
-    correction = jnp.dot(cross, coefficients, precision=highest, preferred_element_type=jnp.float32)
-    return product, (product - correction) / nugget
+    )(index, scalars, *pieces, line_probes)
+
+    panels = rank // PANEL
+    cuts = (panels * 3 // 8, panels * 6 // 8)
+    cost = pl.CostEstimate(flops=4 * rank**3, bytes_accessed=8 * rank**2, transcendentals=0)
+    matrix = jax.ShapeDtypeStruct((rank, rank), jnp.float32)
+
+    def steps(value, first, last):
+        return pl.pallas_call(
+            functools.partial(invert_kernel, first=first, last=last),
+            out_shape=matrix,
+            in_specs=[vmem],
+            out_specs=vmem,
+            cost_estimate=cost,
+            name="steps",
+        )(value)
+
+    arrived = send(outgoing, step_core)
+    inverse = steps(gram, 0, cuts[0])
+    inverse, arrived = lax.optimization_barrier((inverse, arrived))
+    kept = kept + arrived
+    arrived = send(kept[2 * local_rows :], step_x)
+    inverse = steps(inverse, cuts[0], cuts[1])
+    inverse, arrived = lax.optimization_barrier((inverse, arrived))
+    kept = jnp.concatenate(
+        [
+            kept[: 2 * local_rows] + arrived[: 2 * local_rows],
+            kept[4 * local_rows :] + arrived[2 * local_rows :],
+        ]
+    )
+    arrived = send(kept[local_rows:], step_y)
+    weight = pl.pallas_call(
+        functools.partial(weight_kernel, first=cuts[1], last=panels),
+        out_shape=jax.ShapeDtypeStruct(cross.shape, jnp.float32),
+        in_specs=[vmem] * 2,
+        out_specs=vmem,
+        scratch_shapes=[pltpu.VMEM((rank, rank), jnp.float32)],
+        cost_estimate=cost,
+        name="weight",
+    )(inverse, cross)
+    output = jax.ShapeDtypeStruct(probes.shape, jnp.float32)
+    return pl.pallas_call(
+        final_kernel,
+        out_shape=(output, output),
+        in_specs=[smem] + [vmem] * 4,
+        out_specs=(vmem, vmem),
+        name="final",
+    )(scalars, kept, arrived, probes, weight)
 
 
 def plain_tile(row_feats, col_feats):

time: 127 us -> 76.9 us (0.61)
  other arithmetic: 56.1 us -> 2.7 us
  Pallas kernels: 18.4 us -> 35.9 us
  local copies, waits for them, and re-layouts: 10.6 us -> 5.4 us
  waiting for transfers between devices: 22.1 us -> 17.8 us
  matrix products: 2.78 us -> 0 us
  between operations: 3.57 us -> 2.13 us
    another operation x9 -> x0, other arithmetic: 54 us -> none  [the longest x6 34.1 us: small_slice(): factor = jnp.linalg.cholesky(gram)]
    pallas_call x0 -> x4, Pallas kernels: none -> 17.5 us  [the longest x2 11.1 us: steps(): pl.pallas_call(functools.partial(invert_kernel, first=first, last=last),...]
    ppermute x13, waiting for transfers between devices: 22.1 us -> 17.8 us  [exchanged(): return lax.ppermute(value, AXES, [(i, i ^ mask) for i in range(count)])]
    another operation x9 -> x0, local copies, waits for them, and re-layouts: 3.89 us -> none
    another operation x8 -> x0, matrix products: 1.94 us -> none  [the longest x6 1.47 us: small_slice(): coefficients = jax.scipy.linalg.cho_solve((factor, True), projected)]
    unnamed x37 -> x31, local copies, waits for them, and re-layouts: 4.73 us -> 4.56 us
  transfers between devices with their start and end apart: 13 -> 13, of which waited for: 5 -> 5; matrix products, arithmetic and copies ran while one was open for 21% -> 3% of each run, Pallas kernels for 0% -> 20%
where the time goes in v2:
time: 76.9 us; the launch traced here: 76.5 us
  Pallas kernels  35.9 us (47%)
  waiting for transfers between devices  17.8 us (23%)
  starting transfers between devices  12.6 us (16%)
  local copies, waits for them, and re-layouts  5.4 us (7%)
  other arithmetic  2.7 us (4%)
  between operations  2.13 us (3%)
    pallas_call x1, Pallas kernels, small_slice(): pl.pallas_call(tile_kernel, out_shape=(jax.ShapeDtypeStruct((rank, rank),...  18.4 us
    ppermute x13, waiting for transfers between devices, exchanged(): return lax.ppermute(value, AXES, [(i, i ^ mask) for i in range(count)])  17.8 us
    ppermute x13, starting transfers between devices, exchanged(): return lax.ppermute(value, AXES, [(i, i ^ mask) for i in range(count)])  12.6 us
    pallas_call x2, Pallas kernels, steps(): pl.pallas_call(functools.partial(invert_kernel, first=first, last=last),...  11.1 us
    unnamed x31, local copies, waits for them, and re-layouts  4.56 us
    pallas_call x1, Pallas kernels, small_slice(): pl.pallas_call(functools.partial(weight_kernel, first=cuts[1], last=panel...  4.54 us
    pallas_call x1, Pallas kernels, small_slice(): pl.pallas_call(final_kernel, out_shape=(output, output), in_specs=[smem]...  1.88 us
  transfers between devices with their start and end apart: 13, of which 5 were waited for; matrix products, arithmetic and copies ran while one was open for 3% of the time, Pallas kernels for 20%

profile of v2, /device:TPU:0, one launch (start us, length us, event | category | flops | bytes accessed | tf_op | source)
XLA Modules:
  0.0 76.5 jit_solution(5652731550890075217)
XLA Ops:
  0.6 0.9 %constant_dynamic-update-slice_fusion.1 = f32[64,384]{1,0:T(8,128)S(1)} fusion(f32[64,256]{1,0:T(8,128)} %param.5), kind=kLoop, calls=%fused_computation.9 | loop fusion | bytes 131072
  1.5 5.1 %collective-permute-start.2 = (f32[64,384]{1,0:T(8,128)S(1)}, f32[64,384]{1,0:T(8,128)S(1)}, u32[]{:S(2)}, u32[]{:S(2)}) collective-permute-start(f32[64,384]{1,0:T(8,128)S(1)} %constant_dynamic-update-slice_fusion), channel_id=1, source_target_pairs={{0,24},{1,25},{2,26},{3,27},{4,28},{5,29},{6,30},{7,31},{8,16},{9,... | collective-permute-start | bytes 294920 | tf_op jit(solution)/shard_map/ppermute | solution.py:197
  6.6 0.6 collective-permute-start
  7.3 3.1 %collective-permute-done.2 = f32[64,384]{1,0:T(8,128)S(1)} collective-permute-done((f32[64,384]{1,0:T(8,128)S(1)}, f32[64,384]{1,0:T(8,128)S(1)}, u32[]{:S(2)}, u32[]{:S(2)}) %collective-permute-start.2) | collective-permute-done | bytes 98336 | tf_op jit(solution)/shard_map/ppermute | solution.py:197
  10.3 0.6 copy-done.11
  11.0 3.9 %collective-permute-done.1 = f32[64,384]{1,0:T(8,128)S(1)} collective-permute-done((f32[64,384]{1,0:T(8,128)S(1)}, f32[64,384]{1,0:T(8,128)S(1)}, u32[]{:S(2)}, u32[]{:S(2)}) %collective-permute-start.1) | collective-permute-done | bytes 98336 | tf_op jit(solution)/shard_map/ppermute | solution.py:197
  15.0 0.8 %copy-done.10 = f32[64,256]{1,0:T(8,128)S(1)} copy-done((f32[64,256]{1,0:T(8,128)S(1)}, f32[64,256]{1,0:T(8,128)}, u32[]{:S(2)}) %copy-start.10) | copy-done | bytes 65560
  15.9 2.5 %collective-permute-start.5 = (f32[256,256]{1,0:T(8,128)S(1)}, f32[256,256]{1,0:T(8,128)S(1)}, u32[]{:S(2)}, u32[]{:S(2)}) collective-permute-start(f32[256,256]{1,0:T(8,128)S(1)} %pad_maximum_fusion.refs_0_), channel_id=1, source_target_pairs={{0,5},{1,4},{2,7},{3,6},{4,1},{5,0},{6,3},{7,2},{8,13},{9,12},{10,... | collective-permute-start | bytes 786440 | tf_op jit(solution)/shard_map/ppermute | solution.py:197
  19.4 6.6 %collective-permute-done.5.refs_3_ = f32[256,256]{1,0:T(8,128)S(1)} collective-permute-done((f32[256,256]{1,0:T(8,128)S(1)}, f32[256,256]{1,0:T(8,128)S(1)}, u32[]{:S(2)}, u32[]{:S(2)}) %collective-permute-start.5) | collective-permute-done | bytes 262176 | tf_op jit(solution)/shard_map/ppermute | solution.py:197
  26.1 3.9 %collective-permute-done.4.refs_2_ = f32[256,256]{1,0:T(8,128)S(1)} collective-permute-done((f32[256,256]{1,0:T(8,128)S(1)}, f32[256,256]{1,0:T(8,128)S(1)}, u32[]{:S(2)}, u32[]{:S(2)}) %collective-permute-start.4) | collective-permute-done | bytes 262176 | tf_op jit(solution)/shard_map/ppermute | solution.py:197
  32.3 0.7 pad_maximum_fusion.3.scalar_ref
  33.0 0.7 slice-done.1
  33.8 0.7 pad_maximum_fusion.2.refs_8_
  34.5 0.6 copy-done.5
  35.4 0.7 copy-done.8
  36.1 18.4 %tiles.1 = (f32[256,256]{1,0:T(8,128)}, f32[512,128]{1,0:T(8,128)}, f32[512,128]{1,0:T(8,128)}, f32[64,256]{1,0:T(8,128)}) custom-call(s32[256]{0:T(256)} %fusion.1.index_ref, f32[2]{0:T(128)} %pad_maximum_fusion.3.scalar_ref, f32[256,256]{1,0:T(8,128)} %copy-done, f32[256,256]{1,0:T(8,128)} %copy-done.4, f32[256,256]{1,0:T(8,128)} %copy-done.3, ...), custom_call_target="tpu_custom_call" | custom-call | tf_op jit(solution)/shard_map/tiles/pallas_call | solution.py:225
  54.6 5.6 %steps.2.gram_ref = f32[256,256]{1,0:T(8,128)} custom-call(f32[256,256]{1,0:T(8,128)} %get-tuple-element.11.gram_ref), custom_call_target="tpu_custom_call" | custom-call | flops 67108864 | bytes 524288 | tf_op jit(solution)/shard_map/steps/pallas_call | solution.py:248
  60.2 1.6 %collective-permute-start.11 = (f32[384,128]{1,0:T(8,128)S(1)}, f32[384,128]{1,0:T(8,128)S(1)}, u32[]{:S(2)}, u32[]{:S(2)}) collective-permute-start(f32[384,128]{1,0:T(8,128)S(1)} %slice.55), channel_id=1, source_target_pairs={{0,1},{1,0},{2,3},{3,2},{4,5},{5,4},{6,7},{7,6},{8,9},{9,8},{10,11... | collective-permute-start | bytes 589832 | tf_op jit(solution)/shard_map/ppermute | solution.py:197
  61.7 5.5 %steps.3.gram_ref = f32[256,256]{1,0:T(8,128)} custom-call(f32[256,256]{1,0:T(8,128)} %steps.2.gram_ref), custom_call_target="tpu_custom_call" | custom-call | flops 67108864 | bytes 524288 | tf_op jit(solution)/shard_map/steps/pallas_call | solution.py:248
  67.5 1.2 %collective-permute-start.12 = (f32[320,128]{1,0:T(8,128)S(1)}, f32[320,128]{1,0:T(8,128)S(1)}, u32[]{:S(2)}, u32[]{:S(2)}) collective-permute-start(f32[320,128]{1,0:T(8,128)S(1)} %fusion), channel_id=1, source_target_pairs={{0,4},{1,5},{2,6},{3,7},{4,0},{5,1},{6,2},{7,3},{8,12},{9,13},{10,... | collective-permute-start | bytes 491528 | tf_op jit(solution)/shard_map/ppermute | solution.py:197
  68.7 4.5 %weight.1.weight_ref = f32[64,256]{1,0:T(8,128)} custom-call(f32[256,256]{1,0:T(8,128)} %steps.3.gram_ref, f32[64,256]{1,0:T(8,128)} %get-tuple-element.17.cross_ref), custom_call_target="tpu_custom_call" | custom-call | flops 67108864 | bytes 524288 | tf_op jit(solution)/shard_map/weight/pallas_call | solution.py:271
  73.2 0.7 pad_maximum_fusion.1.kept_ref
  73.9 0.7 copy-done.12
  74.6 1.9 %final.1 = (f32[64,128]{1,0:T(8,128)}, f32[64,128]{1,0:T(8,128)}) custom-call(f32[2]{0:T(128)} %pad_maximum_fusion.3.scalar_ref, f32[384,128]{1,0:T(8,128)} %pad_maximum_fusion.1.kept_ref, f32[320,128]{1,0:T(8,128)} %copy-done.12, f32[64,128]{1,0:T(8,128)} %probes_ref.1, f32[64,256]{1,0:T(8,128)} %weight.1.weight_ref), custom_call_target="tpu_custom_call" | custom-call | tf_op jit(solution)/shard_map/final/pallas_call | solution.py:281
  (58 shorter events, 2.9 us)
Async XLA Ops:
  0.6 0.9 %copy-start.1 = (f32[64,128]{1,0:T(8,128)S(1)}, f32[64,128]{1,0:T(8,128)}, u32[]{:S(2)}) copy-start(f32[64,128]{1,0:T(8,128)} %probes_ref.1) | copy-start | bytes 98308
  1.5 8.8 %collective-permute-start.2 = (f32[64,384]{1,0:T(8,128)S(1)}, f32[64,384]{1,0:T(8,128)S(1)}, u32[]{:S(2)}, u32[]{:S(2)}) collective-permute-start(f32[64,384]{1,0:T(8,128)S(1)} %constant_dynamic-update-slice_fusion), channel_id=1, source_target_pairs={{0,24},{1,25},{2,26},{3,27},{4,28},{5,29},{6,30},{7,31},{8,16},{9,... | collective-permute-start | bytes 294920 | tf_op jit(solution)/shard_map/ppermute | solution.py:197
  6.6 8.3 %collective-permute-start.1 = (f32[64,384]{1,0:T(8,128)S(1)}, f32[64,384]{1,0:T(8,128)S(1)}, u32[]{:S(2)}, u32[]{:S(2)}) collective-permute-start(f32[64,384]{1,0:T(8,128)S(1)} %constant_dynamic-update-slice_fusion), channel_id=1, source_target_pairs={{0,16},{1,17},{2,18},{3,19},{4,20},{5,21},{6,22},{7,23},{8,24},{9,... | collective-permute-start | bytes 294920 | tf_op jit(solution)/shard_map/ppermute | solution.py:197
  6.6 8.3 %collective-permute-start = (f32[64,384]{1,0:T(8,128)S(1)}, f32[64,384]{1,0:T(8,128)S(1)}, u32[]{:S(2)}, u32[]{:S(2)}) collective-permute-start(f32[64,384]{1,0:T(8,128)S(1)} %constant_dynamic-update-slice_fusion), channel_id=1, source_target_pairs={{0,8},{1,9},{2,10},{3,11},{4,12},{5,13},{6,14},{7,15},{8,0},{9,1},... | collective-permute-start | bytes 294920 | tf_op jit(solution)/shard_map/ppermute | solution.py:197
  14.9 18.1 %copy-start.13 = (f32[64,384]{1,0:T(8,128)}, f32[64,384]{1,0:T(8,128)S(1)}, u32[]{:S(2)}) copy-start(f32[64,384]{1,0:T(8,128)S(1)} %collective-permute-done.1) | copy-start | bytes 294916
  14.9 0.9 %copy-start.10 = (f32[64,256]{1,0:T(8,128)S(1)}, f32[64,256]{1,0:T(8,128)}, u32[]{:S(2)}) copy-start(f32[64,256]{1,0:T(8,128)} %param.5) | copy-start | bytes 196612
  14.9 0.9 %slice-start = ((f32[64,384]{1,0:T(8,128)}), f32[64,256]{1,0:T(8,128)S(1)}, s32[]{:S(2)}) async-start(f32[64,384]{1,0:T(8,128)} %copy-done.11), calls=%async_computation | async-start | bytes 131072 | tf_op jit(solution)/shard_map/slice | solution.py:216
  15.9 18.6 %copy-start = (f32[256,256]{1,0:T(8,128)}, f32[256,256]{1,0:T(8,128)S(1)}, u32[]{:S(2)}) copy-start(f32[256,256]{1,0:T(8,128)S(1)} %pad_maximum_fusion.refs_0_) | copy-start | bytes 786436
  15.9 10.2 %collective-permute-start.5 = (f32[256,256]{1,0:T(8,128)S(1)}, f32[256,256]{1,0:T(8,128)S(1)}, u32[]{:S(2)}, u32[]{:S(2)}) collective-permute-start(f32[256,256]{1,0:T(8,128)S(1)} %pad_maximum_fusion.refs_0_), channel_id=1, source_target_pairs={{0,5},{1,4},{2,7},{3,6},{4,1},{5,0},{6,3},{7,2},{8,13},{9,12},{10,... | collective-permute-start | bytes 786440 | tf_op jit(solution)/shard_map/ppermute | solution.py:197
  18.4 11.5 %collective-permute-start.4 = (f32[256,256]{1,0:T(8,128)S(1)}, f32[256,256]{1,0:T(8,128)S(1)}, u32[]{:S(2)}, u32[]{:S(2)}) collective-permute-start(f32[256,256]{1,0:T(8,128)S(1)} %pad_maximum_fusion.refs_0_), channel_id=1, source_target_pairs={{0,1},{1,0},{2,3},{3,2},{4,5},{5,4},{6,7},{7,6},{8,9},{9,8},{10,11... | collective-permute-start | bytes 786440 | tf_op jit(solution)/shard_map/ppermute | solution.py:197
  18.9 11.0 %collective-permute-start.3 = (f32[256,256]{1,0:T(8,128)S(1)}, f32[256,256]{1,0:T(8,128)S(1)}, u32[]{:S(2)}, u32[]{:S(2)}) collective-permute-start(f32[256,256]{1,0:T(8,128)S(1)} %pad_maximum_fusion.refs_0_), channel_id=1, source_target_pairs={{0,4},{1,5},{2,6},{3,7},{4,0},{5,1},{6,2},{7,3},{8,12},{9,13},{10,... | collective-permute-start | bytes 786440 | tf_op jit(solution)/shard_map/ppermute | solution.py:197
  19.4 11.0 %copy-start.14 = (s32[256]{0:T(256)S(1)}, s32[256]{0:T(256)}, u32[]{:S(2)}) copy-start(s32[256]{0:T(256)} %param.9) | copy-start | bytes 3076
  19.4 15.0 %collective-permute-start.6 = (f32[256,256]{1,0:T(8,128)S(1)}, f32[256,256]{1,0:T(8,128)S(1)}, u32[]{:S(2)}, u32[]{:S(2)}) collective-permute-start(f32[256,256]{1,0:T(8,128)S(1)} %pad_maximum_fusion.refs_0_), channel_id=1, source_target_pairs={{0,2},{1,3},{2,0},{3,1},{4,6},{5,7},{6,4},{7,5},{8,10},{9,11},{10,... | collective-permute-start | bytes 786440 | tf_op jit(solution)/shard_map/ppermute | solution.py:197
  26.0 8.5 %copy-start.2 = (f32[256,256]{1,0:T(8,128)}, f32[256,256]{1,0:T(8,128)S(1)}, u32[]{:S(2)}) copy-start(f32[256,256]{1,0:T(8,128)S(1)} %collective-permute-done.5.refs_3_) | copy-start | bytes 786436
  26.0 8.4 %collective-permute-start.9 = (f32[256,256]{1,0:T(8,128)S(1)}, f32[256,256]{1,0:T(8,128)S(1)}, u32[]{:S(2)}, u32[]{:S(2)}) collective-permute-start(f32[256,256]{1,0:T(8,128)S(1)} %collective-permute-done.5.refs_3_), channel_id=1, source_target_pairs={{0,2},{1,3},{2,0},{3,1},{4,6},{5,7},{6,4},{7,5},{8,10},{9,11},{10,... | collective-permute-start | bytes 786440 | tf_op jit(solution)/shard_map/ppermute | solution.py:197
  29.9 4.6 %copy-start.3 = (f32[256,256]{1,0:T(8,128)}, f32[256,256]{1,0:T(8,128)S(1)}, u32[]{:S(2)}) copy-start(f32[256,256]{1,0:T(8,128)S(1)} %collective-permute-done.4.refs_2_) | copy-start | bytes 786436
  29.9 4.5 %collective-permute-start.8 = (f32[256,256]{1,0:T(8,128)S(1)}, f32[256,256]{1,0:T(8,128)S(1)}, u32[]{:S(2)}, u32[]{:S(2)}) collective-permute-start(f32[256,256]{1,0:T(8,128)S(1)} %collective-permute-done.4.refs_2_), channel_id=1, source_target_pairs={{0,2},{1,3},{2,0},{3,1},{4,6},{5,7},{6,4},{7,5},{8,10},{9,11},{10,... | collective-permute-start | bytes 786440 | tf_op jit(solution)/shard_map/ppermute | solution.py:197
  29.9 4.6 %copy-start.4 = (f32[256,256]{1,0:T(8,128)}, f32[256,256]{1,0:T(8,128)S(1)}, u32[]{:S(2)}) copy-start(f32[256,256]{1,0:T(8,128)S(1)} %collective-permute-done.3.refs_1_) | copy-start | bytes 786436
  29.9 4.5 %collective-permute-start.7 = (f32[256,256]{1,0:T(8,128)S(1)}, f32[256,256]{1,0:T(8,128)S(1)}, u32[]{:S(2)}, u32[]{:S(2)}) collective-permute-start(f32[256,256]{1,0:T(8,128)S(1)} %collective-permute-done.3.refs_1_), channel_id=1, source_target_pairs={{0,2},{1,3},{2,0},{3,1},{4,6},{5,7},{6,4},{7,5},{8,10},{9,11},{10,... | collective-permute-start | bytes 786440 | tf_op jit(solution)/shard_map/ppermute | solution.py:197
  34.5 0.9 %copy-start.7 = (f32[256,256]{1,0:T(8,128)}, f32[256,256]{1,0:T(8,128)S(1)}, u32[]{:S(2)}) copy-start(f32[256,256]{1,0:T(8,128)S(1)} %collective-permute-done.8.refs_6_) | copy-start | bytes 786436
  54.5 5.7 %collective-permute-start.10 = (f32[512,128]{1,0:T(8,128)}, f32[512,128]{1,0:T(8,128)S(1)}, u32[]{:S(2)}, u32[]{:S(2)}) collective-permute-start(f32[512,128]{1,0:T(8,128)} %get-tuple-element.12), channel_id=1, source_target_pairs={{0,2},{1,3},{2,0},{3,1},{4,6},{5,7},{6,4},{7,5},{8,10},{9,11},{10,... | collective-permute-start | bytes 786440 | tf_op jit(solution)/shard_map/ppermute | solution.py:197
  54.6 5.6 %copy-start.9 = (f32[512,128]{1,0:T(8,128)S(1)}, f32[512,128]{1,0:T(8,128)}, u32[]{:S(2)}) copy-start(f32[512,128]{1,0:T(8,128)} %get-tuple-element.10) | copy-start | bytes 786436
  60.2 7.3 %collective-permute-start.11 = (f32[384,128]{1,0:T(8,128)S(1)}, f32[384,128]{1,0:T(8,128)S(1)}, u32[]{:S(2)}, u32[]{:S(2)}) collective-permute-start(f32[384,128]{1,0:T(8,128)S(1)} %slice.55), channel_id=1, source_target_pairs={{0,1},{1,0},{2,3},{3,2},{4,5},{5,4},{6,7},{7,6},{8,9},{9,8},{10,11... | collective-permute-start | bytes 589832 | tf_op jit(solution)/shard_map/ppermute | solution.py:197
  67.5 6.4 %collective-permute-start.12 = (f32[320,128]{1,0:T(8,128)S(1)}, f32[320,128]{1,0:T(8,128)S(1)}, u32[]{:S(2)}, u32[]{:S(2)}) collective-permute-start(f32[320,128]{1,0:T(8,128)S(1)} %fusion), channel_id=1, source_target_pairs={{0,4},{1,5},{2,6},{3,7},{4,0},{5,1},{6,2},{7,3},{8,12},{9,13},{10,... | collective-permute-start | bytes 491528 | tf_op jit(solution)/shard_map/ppermute | solution.py:197
  (7 other events, 5.1 us)

commit v3 on v2

--- a/solution.py
+++ b/solution.py
@@ -13,91 +13,109 @@
 AXES = ("blk", "row")
 NT = (((1,), (1,)), ((), ()))
 NN = (((1,), (0,)), ((), ()))
-
-
-def split(value):
-    high = value.astype(jnp.bfloat16)
-    low = (value - high.astype(jnp.float32)).astype(jnp.bfloat16)
-    return high, low
-
-
-def dot3(left, right, dims):
-    left_high, left_low = left
-    right_high, right_low = right
-    product = functools.partial(
-        lax.dot_general, dimension_numbers=dims, preferred_element_type=jnp.float32
-    )
-    return (
-        product(left_high, right_low) + product(left_low, right_high) + product(left_high, right_high)
-    )
+vmem = pl.BlockSpec(memory_space=pltpu.VMEM)
+smem = pl.BlockSpec(memory_space=pltpu.SMEM)
+
+
+def split(value, count=2):
+    parts = []
+    for _ in range(count):
+        part = value.astype(jnp.bfloat16)
+        parts.append(part)
+        if len(parts) < count:
+            value = value - part.astype(jnp.float32)
+    return parts
+
+
+def dot(left, right, dims):
+    return lax.dot_general(left, right, dims, preferred_element_type=jnp.float32)
 
 
 def dot6(left, right, dims):
     return lax.dot_general(left, right, dims, precision=highest, preferred_element_type=jnp.float32)
 
 
-def matern(row_feats, row_norms, col_feats, col_norms):
-    five_squared = dot6(row_feats, col_feats, NT) + row_norms + col_norms
+def dot3(left, right, dims):
+    return dot(left[0], right[1], dims) + dot(left[1], right[0], dims) + dot(left[0], right[0], dims)
+
+
+def row_side(value):
+    high, mid = split(value)
+    return jnp.concatenate([mid, mid, high, high], axis=1)
+
+
+def col_side(value):
+    high, mid = split(value)
+    return jnp.concatenate([mid, high, mid, high], axis=1)
+
+
+def matern(row_wide, row_norms, col_wide, col_norms):
+    five_squared = dot(row_wide, col_wide, NT) + row_norms + col_norms
     five_squared = jnp.maximum(five_squared, tiny)
     scaled = five_squared * lax.rsqrt(five_squared)
     return (1.0 + scaled + five_squared * (1.0 / 3.0)) * jnp.exp(-scaled)
 
 
-def lane_norms(feats):
-    ones = jnp.full((8, feats.shape[1]), 5.0, jnp.float32)
-    return dot6(ones, feats * feats, NT)[0:1, :]
-
-
-def tile_kernel(index_ref, scalar_ref, *refs):
+def sums(feats):
+    return 5.0 * jnp.sum(feats * feats, axis=1, keepdims=True)
+
+
+def flipped(column):
+    return jnp.transpose(jnp.broadcast_to(column, (column.shape[0], 128)))[0:1, :]
+
+
+def tile_kernel(index_ref, scale_ref, noise_ref, *refs):
     pieces = refs[:8]
-    probes_ref, gram_ref, send_ref, keep_ref, cross_ref, all_ref, query_ref = refs[8:]
+    (probes_ref, gram_ref, send_ref, keep_ref, cross_ref, all_ref, query_ref,
+     wide_ref, high_ref, low_ref) = refs[8:]
     line_rows, feature_count = pieces[0].shape
     rank = gram_ref.shape[0]
     local_rows = cross_ref.shape[0]
-    amplitude = scalar_ref[0]
-    nugget = scalar_ref[1]
+    amplitude = scale_ref[0]
+    nugget = noise_ref[0]
     for position, piece in enumerate(pieces):
         all_ref[position * line_rows : (position + 1) * line_rows, :] = piece[:, :]
-
     def pick(step, carry):
         query_ref[pl.ds(step, 1), :] = all_ref[pl.ds(index_ref[step], 1), :]
         return carry
-
     lax.fori_loop(0, rank, pick, 0, unroll=8)
-    pivot_feats = query_ref[:rank, :]
+    pivot_feats = query_ref[:, :]
     line_feats = pieces[0][:, :]
-    query_ref[rank:, :] = line_feats
-    query = query_ref[:, :]
-    query_norms = 5.0 * jnp.sum(query * query, axis=1, keepdims=True)
-    query_scaled = -10.0 * query
-    pivot_norms = lane_norms(pivot_feats)
-    line_norms = lane_norms(line_feats)
+    pivot_sums = sums(pivot_feats)
+    line_sums = sums(line_feats)
+    query_sums = jnp.concatenate([pivot_sums, line_sums], axis=0)
+    pivot_flipped = flipped(pivot_sums)
+    line_flipped = flipped(line_sums)
+    wide_ref[:rank, :] = row_side(-10.0 * pivot_feats)
+    wide_ref[rank:, :] = row_side(-10.0 * line_feats)
+    line_wide = col_side(line_feats)
+    pivot_wide = col_side(pivot_feats)
     probes = split(probes_ref[:, :])
-    total = None
-    line_cross = None
+    own = jnp.concatenate([piece[:local_rows, :] for piece in pieces], axis=0)
+    own_wide = row_side(-10.0 * own)
+    own_sums = sums(own)
+    rows = dot3(split(matern(own_wide, own_sums, line_wide, line_flipped)), probes, NN)
+    keep_ref[: 4 * local_rows, :] = rows[: 4 * local_rows, :]
+    send_ref[: 4 * local_rows, :] = rows[4 * local_rows :, :]
+    cross_ref[:, :] = amplitude * matern(own_wide[:local_rows], own_sums[:local_rows], pivot_wide, pivot_flipped)
     for position, piece in enumerate(pieces):
         feats = piece[:, :]
-        tile = matern(query_scaled, query_norms, feats, lane_norms(feats))
-        halves = split(tile)
-        part = dot3((halves[0][:rank], halves[1][:rank]), halves, NT)
-        total = part if total is None else total + part
+        feat_sums = sums(feats) if position else line_sums
+        wide = [wide_ref[:rank, :], wide_ref[rank:, :]]; col = col_side(feats) if position else line_wide; fl=flipped(feat_sums)
+        tile = jnp.concatenate([matern(wide[0], pivot_sums, col, fl), matern(wide[1], line_sums, col, fl)], axis=0)
+        span = slice(position * line_rows, (position + 1) * line_rows)
+        high, low = split(tile)
+        high_ref[:, span] = high
+        low_ref[:, span] = low
         if position == 0:
             line_cross = tile[:rank, :]
-        own = feats[:local_rows, :]
-        own_norms = 5.0 * jnp.sum(own * own, axis=1, keepdims=True)
-        own_tile = matern(-10.0 * own, own_norms, line_feats, line_norms)
-        rows = dot3(split(own_tile), probes, NN)
-        if position < 4:
-            keep_ref[position * local_rows : (position + 1) * local_rows, :] = rows
-        else:
-            send_ref[(position - 4) * local_rows : (position - 3) * local_rows, :] = rows
-        if position == 0:
-            cross_ref[:, :] = amplitude * matern(-10.0 * own, own_norms, pivot_feats, pivot_norms)
-    inner = matern(query_scaled[:rank], query_norms[:rank], pivot_feats, pivot_norms)
+    inner = matern(wide_ref[:rank, :], pivot_sums, pivot_wide, pivot_flipped)
     square = amplitude * amplitude
-    gram_ref[:, :] = (nugget * amplitude) * inner + square * total[:, :rank]
-    mixed = square * total[:, rank:] + (nugget * amplitude) * line_cross
-    projected = dot3(split(mixed), probes, NN)
+    left_high, left_low = high_ref[:, :], low_ref[:, :]
+    total = dot3((left_high, left_low), (left_high[:rank], left_low[:rank]), NT)
+    gram_ref[:, :] = (nugget * amplitude) * inner + square * total[:rank, :]
+    mixed = square * total[rank:, :] + (nugget * amplitude) * jnp.transpose(line_cross)
+    projected = dot3(split(jnp.transpose(mixed)), probes, NN)
     keep_ref[4 * local_rows :, :] = projected
     send_ref[4 * local_rows :, :] = projected
 
@@ -182,15 +200,29 @@
     out_ref[:, :] = dot6(cross_ref[:, :], work_ref[:, :], NN)
 
 
-def final_kernel(scalar_ref, kept_ref, arrived_ref, probes_ref, weight_ref, product_ref, out_ref):
+def final_kernel(scale_ref, noise_ref, kept_ref, arrived_ref, probes_ref, weight_ref, product_ref, out_ref):
     local_rows = probes_ref.shape[0]
-    nugget = scalar_ref[1]
+    nugget = noise_ref[0]
     kernel_probes = kept_ref[:local_rows, :] + arrived_ref[:local_rows, :]
     projected = kept_ref[2 * local_rows :, :] + arrived_ref[local_rows:, :]
-    product = scalar_ref[0] * kernel_probes + nugget * probes_ref[:, :]
+    product = scale_ref[0] * kernel_probes + nugget * probes_ref[:, :]
     product_ref[:, :] = product
     correction = dot6(weight_ref[:, :], projected, NN)
     out_ref[:, :] = (product - correction) * (1.0 / nugget)
+
+
+def near(value):
+    return pltpu.with_memory_space_constraint(value, pltpu.VMEM)
+
+
+def assemble_kernel(*refs):
+    parts, (feats_ref, probes_ref) = refs[:4], refs[4:]
+    rows = parts[0].shape[0]
+    feature_count = feats_ref.shape[1]
+    for position, part in enumerate(parts):
+        span = slice(position * rows, (position + 1) * rows)
+        feats_ref[span, :] = part[:, :feature_count]
+        probes_ref[span, :] = part[:, feature_count:]
 
 
 def exchanged(value, mask, count):
@@ -213,36 +245,48 @@
 
     packed = jnp.concatenate([features, probes], axis=1)
     line = [packed] + [send(packed, step_z * step) for step in (1, 2, 3)]
-    line_feats = jnp.concatenate([part[:, :feature_count] for part in line], axis=0)
-    line_probes = jnp.concatenate([part[:, feature_count:] for part in line], axis=0)
-    pieces = [line_feats] + [send(line_feats, mask) for mask in (step_y, step_x, step_x + step_y)]
+    line_rows = 4 * local_rows
+    line_feats, line_probes = pl.pallas_call(
+        assemble_kernel,
+        out_shape=(
+            pltpu.VMEM((line_rows, feature_count), jnp.float32),
+            pltpu.VMEM((line_rows, probe_count), jnp.float32),
+        ),
+        in_specs=[vmem] * 4,
+        out_specs=(vmem,) * 2,
+        name="assemble",
+    )(*[near(part) for part in line])
+    arrived = [send(line_feats, mask) for mask in (step_y, step_x, step_x + step_y)]
+    arrived[0], index = lax.optimization_barrier((arrived[0], index))
+    pieces = [line_feats] + arrived
     pieces = pieces + [send(piece, step_core) for piece in pieces]
 
-    scalars = jnp.concatenate([outputscale, noise])
-    vmem = pl.BlockSpec(memory_space=pltpu.VMEM)
-    smem = pl.BlockSpec(memory_space=pltpu.SMEM)
-    half = 4 * local_rows + rank
+    half = line_rows + rank
+    wide = line_rows + rank
     gram, outgoing, kept, cross = pl.pallas_call(
         tile_kernel,
         out_shape=(
-            jax.ShapeDtypeStruct((rank, rank), jnp.float32),
-            jax.ShapeDtypeStruct((half, probe_count), jnp.float32),
-            jax.ShapeDtypeStruct((half, probe_count), jnp.float32),
-            jax.ShapeDtypeStruct((local_rows, rank), jnp.float32),
+            pltpu.VMEM((rank, rank), jnp.float32),
+            pltpu.VMEM((half, probe_count), jnp.float32),
+            pltpu.VMEM((half, probe_count), jnp.float32),
+            pltpu.VMEM((local_rows, rank), jnp.float32),
         ),
-        in_specs=[smem, smem] + [vmem] * 9,
+        in_specs=[smem] * 3 + [vmem] * 9,
         out_specs=(vmem,) * 4,
         scratch_shapes=[
-            pltpu.VMEM((8 * 4 * local_rows, feature_count), jnp.float32),
-            pltpu.VMEM((rank + 4 * local_rows, feature_count), jnp.float32),
+            pltpu.VMEM((8 * line_rows, feature_count), jnp.float32),
+            pltpu.VMEM((rank, feature_count), jnp.float32),
+            pltpu.VMEM((wide, 4 * feature_count), jnp.bfloat16),
+            pltpu.VMEM((wide, 8 * line_rows), jnp.bfloat16),
+            pltpu.VMEM((wide, 8 * line_rows), jnp.bfloat16),
         ],
         name="tiles",
-    )(index, scalars, *pieces, line_probes)
+    )(index, outputscale, noise, *[near(piece) for piece in pieces], near(line_probes))
 
     panels = rank // PANEL
     cuts = (panels * 3 // 8, panels * 6 // 8)
     cost = pl.CostEstimate(flops=4 * rank**3, bytes_accessed=8 * rank**2, transcendentals=0)
-    matrix = jax.ShapeDtypeStruct((rank, rank), jnp.float32)
+    matrix = pltpu.VMEM((rank, rank), jnp.float32)
 
     def steps(value, first, last):
         return pl.pallas_call(
@@ -252,7 +296,7 @@
             out_specs=vmem,
             cost_estimate=cost,
             name="steps",
-        )(value)
+        )(near(value))
 
     arrived = send(outgoing, step_core)
     inverse = steps(gram, 0, cuts[0])
@@ -270,27 +314,29 @@
     arrived = send(kept[local_rows:], step_y)
     weight = pl.pallas_call(
         functools.partial(weight_kernel, first=cuts[1], last=panels),
-        out_shape=jax.ShapeDtypeStruct(cross.shape, jnp.float32),
+        out_shape=pltpu.VMEM(cross.shape, jnp.float32),
         in_specs=[vmem] * 2,
         out_specs=vmem,
         scratch_shapes=[pltpu.VMEM((rank, rank), jnp.float32)],
         cost_estimate=cost,
         name="weight",
-    )(inverse, cross)
+    )(near(inverse), near(cross))
     output = jax.ShapeDtypeStruct(probes.shape, jnp.float32)
     return pl.pallas_call(
         final_kernel,
         out_shape=(output, output),
-        in_specs=[smem] + [vmem] * 4,
+        in_specs=[smem] * 2 + [vmem] * 4,
         out_specs=(vmem, vmem),
         name="final",
-    )(scalars, kept, arrived, probes, weight)
+    )(outputscale, noise, near(kept), near(arrived), probes, near(weight))
 
 
 def plain_tile(row_feats, col_feats):
-    row_norms = 5.0 * jnp.sum(row_feats * row_feats, axis=1)[:, None]
-    col_norms = 5.0 * jnp.sum(col_feats * col_feats, axis=1)[None, :]
-    return matern(-10.0 * row_feats, row_norms, col_feats, col_norms)
+    row_norms = jnp.sum(row_feats * row_feats, axis=1)[:, None]
+    col_norms = jnp.sum(col_feats * col_feats, axis=1)[None, :]
+    inner = dot6(row_feats, col_feats, NT)
+    scaled = root_five * jnp.sqrt(jnp.maximum(row_norms + col_norms - 2.0 * inner, 0.0))
+    return (1.0 + scaled + scaled * scaled / 3.0) * jnp.exp(-scaled)
 
 
 def large_slice(features, probes, outputscale, noise, pivots):

time: 76.9 us -> 58 us (0.75)
  Pallas kernels: 35.9 us -> 20.1 us
  local copies, waits for them, and re-layouts: 5.4 us -> 1.55 us
  waiting for transfers between devices: 17.8 us -> 20.1 us
  other arithmetic: 2.7 us -> 0.67 us
    pallas_call x1 -> x2, Pallas kernels: 18.4 us -> 7.99 us  [the longest x1 7.96 us: small_slice(): pl.pallas_call(tile_kernel, out_shape=(pltpu.VMEM((rank, rank), jnp.float...]
    pallas_call x2, Pallas kernels: 11.1 us -> 7.55 us  [steps(): pl.pallas_call(functools.partial(invert_kernel, first=first, last=last),...]
    unnamed x31 -> x5, local copies, waits for them, and re-layouts: 4.56 us -> 1.54 us
    ppermute x13, waiting for transfers between devices: 17.8 us -> 20.1 us  [exchanged(): return lax.ppermute(value, AXES, [(i, i ^ mask) for i in range(count)])]
    pallas_call x1, Pallas kernels: 4.54 us -> 2.97 us  [small_slice(): pl.pallas_call(functools.partial(weight_kernel, first=cuts[1], last=panel...]
    concatenate x3 -> x0, other arithmetic: 1.35 us -> none  [the longest x1 0.67 us: small_slice(): jnp.concatenate([part[:, feature_count:] for part in line], axis=0)]
    slice x9 -> x0, local copies, waits for them, and re-layouts: 0.81 us -> none  [the longest x5 0.77 us: small_slice(): part[:, feature_count:]]
  transfers between devices with their start and end apart: 13 -> 13, of which waited for: 5 -> 7; matrix products, arithmetic and copies ran while one was open for 3% -> 1% of each run, Pallas kernels for 20% -> 18%
where the time goes in v3:
time: 58 us; the launch traced here: 57.7 us
  waiting for transfers between devices  20.1 us (35%)
  Pallas kernels  20.1 us (35%)
  starting transfers between devices  13.2 us (23%)
  between operations  2.06 us (4%)
  local copies, waits for them, and re-layouts  1.55 us (3%)
  other arithmetic  0.67 us (1%)
    ppermute x13, waiting for transfers between devices, exchanged(): return lax.ppermute(value, AXES, [(i, i ^ mask) for i in range(count)])  20.1 us
    ppermute x13, starting transfers between devices, exchanged(): return lax.ppermute(value, AXES, [(i, i ^ mask) for i in range(count)])  13.2 us
    pallas_call x1, Pallas kernels, small_slice(): pl.pallas_call(tile_kernel, out_shape=(pltpu.VMEM((rank, rank), jnp.float...  7.96 us
    pallas_call x2, Pallas kernels, steps(): pl.pallas_call(functools.partial(invert_kernel, first=first, last=last),...  7.55 us
    pallas_call x1, Pallas kernels, small_slice(): pl.pallas_call(functools.partial(weight_kernel, first=cuts[1], last=panel...  2.97 us
    pallas_call x1, Pallas kernels, small_slice(): pl.pallas_call(final_kernel, out_shape=(output, output), in_specs=[smem]...  1.6 us
    unnamed x5, local copies, waits for them, and re-layouts  1.54 us
  transfers between devices with their start and end apart: 13, of which 7 were waited for; matrix products, arithmetic and copies ran while one was open for 1% of the time, Pallas kernels for 18%

profile of v3, /device:TPU:0, one launch (start us, length us, event | category | flops | bytes accessed | tf_op | source)
XLA Modules:
  0.0 57.7 jit_solution(10795751210622568663)
XLA Ops:
  0.6 0.9 %constant_dynamic-update-slice_fusion.1 = f32[64,384]{1,0:T(8,128)S(1)} fusion(f32[64,256]{1,0:T(8,128)} %param.5), kind=kLoop, calls=%fused_computation.7 | loop fusion | bytes 131072
  1.5 5.1 %collective-permute-start.2 = (f32[64,384]{1,0:T(8,128)S(1)}, f32[64,384]{1,0:T(8,128)S(1)}, u32[]{:S(2)}, u32[]{:S(2)}) collective-permute-start(f32[64,384]{1,0:T(8,128)S(1)} %constant_dynamic-update-slice_fusion.refs_0_), channel_id=1, source_target_pairs={{0,24},{1,25},{2,26},{3,27},{4,28},{5,29},{6,30},{7,31},{8,16},{9,... | collective-permute-start | bytes 294920 | tf_op jit(solution)/shard_map/ppermute | solution.py:229
  6.6 0.6 %collective-permute-start = (f32[64,384]{1,0:T(8,128)S(1)}, f32[64,384]{1,0:T(8,128)S(1)}, u32[]{:S(2)}, u32[]{:S(2)}) collective-permute-start(f32[64,384]{1,0:T(8,128)S(1)} %constant_dynamic-update-slice_fusion.refs_0_), channel_id=1, source_target_pairs={{0,8},{1,9},{2,10},{3,11},{4,12},{5,13},{6,14},{7,15},{8,0},{9,1},... | collective-permute-start | bytes 294920 | tf_op jit(solution)/shard_map/ppermute | solution.py:229
  7.3 3.1 %collective-permute-done.2.refs_3_ = f32[64,384]{1,0:T(8,128)S(1)} collective-permute-done((f32[64,384]{1,0:T(8,128)S(1)}, f32[64,384]{1,0:T(8,128)S(1)}, u32[]{:S(2)}, u32[]{:S(2)}) %collective-permute-start.2) | collective-permute-done | bytes 98336 | tf_op jit(solution)/shard_map/ppermute | solution.py:229
  10.3 4.6 %collective-permute-done.1.refs_2_ = f32[64,384]{1,0:T(8,128)S(1)} collective-permute-done((f32[64,384]{1,0:T(8,128)S(1)}, f32[64,384]{1,0:T(8,128)S(1)}, u32[]{:S(2)}, u32[]{:S(2)}) %collective-permute-start.1) | collective-permute-done | bytes 98336 | tf_op jit(solution)/shard_map/ppermute | solution.py:229
  14.9 1.6 %collective-permute-start.3 = (f32[256,256]{1,0:T(8,128)S(1)}, f32[256,256]{1,0:T(8,128)S(1)}, u32[]{:S(2)}, u32[]{:S(2)}) collective-permute-start(f32[256,256]{1,0:T(8,128)S(1)} %get-tuple-element.14.refs_0_), channel_id=1, source_target_pairs={{0,4},{1,5},{2,6},{3,7},{4,0},{5,1},{6,2},{7,3},{8,12},{9,13},{10,... | collective-permute-start | bytes 786440 | tf_op jit(solution)/shard_map/ppermute | solution.py:229
  16.5 1.4 %collective-permute-start.5 = (f32[256,256]{1,0:T(8,128)S(1)}, f32[256,256]{1,0:T(8,128)S(1)}, u32[]{:S(2)}, u32[]{:S(2)}) collective-permute-start(f32[256,256]{1,0:T(8,128)S(1)} %get-tuple-element.14.refs_0_), channel_id=1, source_target_pairs={{0,5},{1,4},{2,7},{3,6},{4,1},{5,0},{6,3},{7,2},{8,13},{9,12},{10,... | collective-permute-start | bytes 786440 | tf_op jit(solution)/shard_map/ppermute | solution.py:229
  18.0 0.5 collective-permute-start.4
  18.5 0.7 %copy-done.1 = s32[256]{0:T(256)S(1)} copy-done((s32[256]{0:T(256)S(1)}, s32[256]{0:T(256)}, u32[]{:S(2)}) %copy-start.1) | copy-done | bytes 1048
  19.2 0.6 %fusion.1.index_ref = s32[256]{0:T(256)} fusion(s32[256]{0:T(256)S(1)} %copy-done.1, s32[]{:T(128)S(6)} %add.34), kind=kLoop, calls=%fused_computation.23 | loop fusion | flops 16896 | bytes 2052 | tf_op jit(solution)/shard_map/add | solution.py:244
  19.8 8.2 %collective-permute-done.3.refs_1_ = f32[256,256]{1,0:T(8,128)S(1)} collective-permute-done((f32[256,256]{1,0:T(8,128)S(1)}, f32[256,256]{1,0:T(8,128)S(1)}, u32[]{:S(2)}, u32[]{:S(2)}) %collective-permute-start.3) | collective-permute-done | bytes 262176 | tf_op jit(solution)/shard_map/ppermute | solution.py:229
  28.0 1.2 %collective-permute-done.4.refs_2_ = f32[256,256]{1,0:T(8,128)S(1)} collective-permute-done((f32[256,256]{1,0:T(8,128)S(1)}, f32[256,256]{1,0:T(8,128)S(1)}, u32[]{:S(2)}, u32[]{:S(2)}) %collective-permute-start.4) | collective-permute-done | bytes 262176 | tf_op jit(solution)/shard_map/ppermute | solution.py:229
  29.2 0.5 collective-permute-start.7
  31.1 0.1 collective-permute-done.7.refs_5_
  31.1 8.0 %tiles.1 = (f32[256,256]{1,0:T(8,128)S(1)}, f32[512,128]{1,0:T(8,128)S(1)}, f32[512,128]{1,0:T(8,128)S(1)}, f32[64,256]{1,0:T(8,128)S(1)}) custom-call(s32[256]{0:T(256)} %fusion.1.index_ref, f32[1]{0:T(128)S(6)} %copy.8.scale_ref, f32[1]{0:T(128)S(6)} %copy.9.noise_ref, f32[256,256]{1,0:T(8,128)S(1)} %get-tuple-element.14.refs_0_, ...), custom_call_target="tpu_custom_call" | custom-call | tf_op jit(solution)/shard_map/tiles/pallas_call | solution.py:266
  39.1 0.2 collective-permute-start.10
  39.3 3.7 %steps.2.gram_ref = f32[256,256]{1,0:T(8,128)S(1)} custom-call(f32[256,256]{1,0:T(8,128)S(1)} %get-tuple-element.19.gram_ref), custom_call_target="tpu_custom_call" | custom-call | flops 67108864 | bytes 524288 | tf_op jit(solution)/shard_map/steps/pallas_call | solution.py:292
  43.1 1.6 %collective-permute-start.11 = (f32[384,128]{1,0:T(8,128)S(1)}, f32[384,128]{1,0:T(8,128)S(1)}, u32[]{:S(2)}, u32[]{:S(2)}) collective-permute-start(f32[384,128]{1,0:T(8,128)S(1)} %slice.25), channel_id=1, source_target_pairs={{0,1},{1,0},{2,3},{3,2},{4,5},{5,4},{6,7},{7,6},{8,9},{9,8},{10,11... | collective-permute-start | bytes 589832 | tf_op jit(solution)/shard_map/ppermute | solution.py:229
  44.7 3.8 %steps.3.gram_ref = f32[256,256]{1,0:T(8,128)S(1)} custom-call(f32[256,256]{1,0:T(8,128)S(1)} %steps.2.gram_ref), custom_call_target="tpu_custom_call" | custom-call | flops 67108864 | bytes 524288 | tf_op jit(solution)/shard_map/steps/pallas_call | solution.py:292
  48.5 1.8 %collective-permute-done.11 = f32[384,128]{1,0:T(8,128)S(1)} collective-permute-done((f32[384,128]{1,0:T(8,128)S(1)}, f32[384,128]{1,0:T(8,128)S(1)}, u32[]{:S(2)}, u32[]{:S(2)}) %collective-permute-start.11) | collective-permute-done | bytes 196640 | tf_op jit(solution)/shard_map/ppermute | solution.py:229
  50.4 1.6 %collective-permute-start.12 = (f32[320,128]{1,0:T(8,128)S(1)}, f32[320,128]{1,0:T(8,128)S(1)}, u32[]{:S(2)}, u32[]{:S(2)}) collective-permute-start(f32[320,128]{1,0:T(8,128)S(1)} %fusion), channel_id=1, source_target_pairs={{0,4},{1,5},{2,6},{3,7},{4,0},{5,1},{6,2},{7,3},{8,12},{9,13},{10,... | collective-permute-start | bytes 491528 | tf_op jit(solution)/shard_map/ppermute | solution.py:229
  52.0 3.0 %weight.1.weight_ref = f32[64,256]{1,0:T(8,128)S(1)} custom-call(f32[256,256]{1,0:T(8,128)S(1)} %steps.3.gram_ref, f32[64,256]{1,0:T(8,128)S(1)} %get-tuple-element.25.cross_ref), custom_call_target="tpu_custom_call" | custom-call | flops 67108864 | bytes 524288 | tf_op jit(solution)/shard_map/weight/pallas_call | solution.py:315
  55.0 1.1 %collective-permute-done.12.arrived_ref = f32[320,128]{1,0:T(8,128)S(1)} collective-permute-done((f32[320,128]{1,0:T(8,128)S(1)}, f32[320,128]{1,0:T(8,128)S(1)}, u32[]{:S(2)}, u32[]{:S(2)}) %collective-permute-start.12) | collective-permute-done | bytes 163872 | tf_op jit(solution)/shard_map/ppermute | solution.py:229
  56.1 1.6 %final.1 = (f32[64,128]{1,0:T(8,128)}, f32[64,128]{1,0:T(8,128)}) custom-call(f32[1]{0:T(128)S(6)} %copy.8.scale_ref, f32[1]{0:T(128)S(6)} %copy.9.noise_ref, f32[384,128]{1,0:T(8,128)S(1)} %pad_maximum_fusion.kept_ref, f32[320,128]{1,0:T(8,128)S(1)} %collective-permute-done.12.arrived_ref, f32[64,128]{1,0:T(8,128)} %probes_ref.1, ...), custom_call_target="tpu_custom_call" | custom-call | tf_op jit(solution)/shard_map/final/pallas_call | solution.py:325
  (21 shorter events, 0.2 us)
Async XLA Ops:
  0.6 0.9 %copy-start = (f32[64,128]{1,0:T(8,128)S(1)}, f32[64,128]{1,0:T(8,128)}, u32[]{:S(2)}) copy-start(f32[64,128]{1,0:T(8,128)} %probes_ref.1) | copy-start | bytes 98308
  1.5 8.8 %collective-permute-start.2 = (f32[64,384]{1,0:T(8,128)S(1)}, f32[64,384]{1,0:T(8,128)S(1)}, u32[]{:S(2)}, u32[]{:S(2)}) collective-permute-start(f32[64,384]{1,0:T(8,128)S(1)} %constant_dynamic-update-slice_fusion.refs_0_), channel_id=1, source_target_pairs={{0,24},{1,25},{2,26},{3,27},{4,28},{5,29},{6,30},{7,31},{8,16},{9,... | collective-permute-start | bytes 294920 | tf_op jit(solution)/shard_map/ppermute | solution.py:229
  6.6 8.3 %collective-permute-start.1 = (f32[64,384]{1,0:T(8,128)S(1)}, f32[64,384]{1,0:T(8,128)S(1)}, u32[]{:S(2)}, u32[]{:S(2)}) collective-permute-start(f32[64,384]{1,0:T(8,128)S(1)} %constant_dynamic-update-slice_fusion.refs_0_), channel_id=1, source_target_pairs={{0,16},{1,17},{2,18},{3,19},{4,20},{5,21},{6,22},{7,23},{8,24},{9,... | collective-permute-start | bytes 294920 | tf_op jit(solution)/shard_map/ppermute | solution.py:229
  6.6 8.3 %collective-permute-start = (f32[64,384]{1,0:T(8,128)S(1)}, f32[64,384]{1,0:T(8,128)S(1)}, u32[]{:S(2)}, u32[]{:S(2)}) collective-permute-start(f32[64,384]{1,0:T(8,128)S(1)} %constant_dynamic-update-slice_fusion.refs_0_), channel_id=1, source_target_pairs={{0,8},{1,9},{2,10},{3,11},{4,12},{5,13},{6,14},{7,15},{8,0},{9,1},... | collective-permute-start | bytes 294920 | tf_op jit(solution)/shard_map/ppermute | solution.py:229
  14.9 13.1 %collective-permute-start.3 = (f32[256,256]{1,0:T(8,128)S(1)}, f32[256,256]{1,0:T(8,128)S(1)}, u32[]{:S(2)}, u32[]{:S(2)}) collective-permute-start(f32[256,256]{1,0:T(8,128)S(1)} %get-tuple-element.14.refs_0_), channel_id=1, source_target_pairs={{0,4},{1,5},{2,6},{3,7},{4,0},{5,1},{6,2},{7,3},{8,12},{9,13},{10,... | collective-permute-start | bytes 786440 | tf_op jit(solution)/shard_map/ppermute | solution.py:229
  16.5 11.5 %collective-permute-start.5 = (f32[256,256]{1,0:T(8,128)S(1)}, f32[256,256]{1,0:T(8,128)S(1)}, u32[]{:S(2)}, u32[]{:S(2)}) collective-permute-start(f32[256,256]{1,0:T(8,128)S(1)} %get-tuple-element.14.refs_0_), channel_id=1, source_target_pairs={{0,5},{1,4},{2,7},{3,6},{4,1},{5,0},{6,3},{7,2},{8,13},{9,12},{10,... | collective-permute-start | bytes 786440 | tf_op jit(solution)/shard_map/ppermute | solution.py:229
  18.0 11.3 %collective-permute-start.4 = (f32[256,256]{1,0:T(8,128)S(1)}, f32[256,256]{1,0:T(8,128)S(1)}, u32[]{:S(2)}, u32[]{:S(2)}) collective-permute-start(f32[256,256]{1,0:T(8,128)S(1)} %get-tuple-element.14.refs_0_), channel_id=1, source_target_pairs={{0,1},{1,0},{2,3},{3,2},{4,5},{5,4},{6,7},{7,6},{8,9},{9,8},{10,11... | collective-permute-start | bytes 786440 | tf_op jit(solution)/shard_map/ppermute | solution.py:229
  18.5 0.7 %copy-start.1 = (s32[256]{0:T(256)S(1)}, s32[256]{0:T(256)}, u32[]{:S(2)}) copy-start(s32[256]{0:T(256)} %param.9) | copy-start | bytes 3076
  19.8 11.3 %collective-permute-start.6 = (f32[256,256]{1,0:T(8,128)S(1)}, f32[256,256]{1,0:T(8,128)S(1)}, u32[]{:S(2)}, u32[]{:S(2)}) collective-permute-start(f32[256,256]{1,0:T(8,128)S(1)} %get-tuple-element.14.refs_0_), channel_id=1, source_target_pairs={{0,2},{1,3},{2,0},{3,1},{4,6},{5,7},{6,4},{7,5},{8,10},{9,11},{10,... | collective-permute-start | bytes 786440 | tf_op jit(solution)/shard_map/ppermute | solution.py:229
  28.0 3.1 %collective-permute-start.9 = (f32[256,256]{1,0:T(8,128)S(1)}, f32[256,256]{1,0:T(8,128)S(1)}, u32[]{:S(2)}, u32[]{:S(2)}) collective-permute-start(f32[256,256]{1,0:T(8,128)S(1)} %collective-permute-done.5.refs_3_), channel_id=1, source_target_pairs={{0,2},{1,3},{2,0},{3,1},{4,6},{5,7},{6,4},{7,5},{8,10},{9,11},{10,... | collective-permute-start | bytes 786440 | tf_op jit(solution)/shard_map/ppermute | solution.py:229
  29.2 1.8 %collective-permute-start.8 = (f32[256,256]{1,0:T(8,128)S(1)}, f32[256,256]{1,0:T(8,128)S(1)}, u32[]{:S(2)}, u32[]{:S(2)}) collective-permute-start(f32[256,256]{1,0:T(8,128)S(1)} %collective-permute-done.4.refs_2_), channel_id=1, source_target_pairs={{0,2},{1,3},{2,0},{3,1},{4,6},{5,7},{6,4},{7,5},{8,10},{9,11},{10,... | collective-permute-start | bytes 786440 | tf_op jit(solution)/shard_map/ppermute | solution.py:229
  29.2 1.9 %collective-permute-start.7 = (f32[256,256]{1,0:T(8,128)S(1)}, f32[256,256]{1,0:T(8,128)S(1)}, u32[]{:S(2)}, u32[]{:S(2)}) collective-permute-start(f32[256,256]{1,0:T(8,128)S(1)} %collective-permute-done.3.refs_1_), channel_id=1, source_target_pairs={{0,2},{1,3},{2,0},{3,1},{4,6},{5,7},{6,4},{7,5},{8,10},{9,11},{10,... | collective-permute-start | bytes 786440 | tf_op jit(solution)/shard_map/ppermute | solution.py:229
  39.1 3.9 %collective-permute-start.10 = (f32[512,128]{1,0:T(8,128)S(1)}, f32[512,128]{1,0:T(8,128)S(1)}, u32[]{:S(2)}, u32[]{:S(2)}) collective-permute-start(f32[512,128]{1,0:T(8,128)S(1)} %get-tuple-element.20), channel_id=1, source_target_pairs={{0,2},{1,3},{2,0},{3,1},{4,6},{5,7},{6,4},{7,5},{8,10},{9,11},{10,... | collective-permute-start | bytes 786440 | tf_op jit(solution)/shard_map/ppermute | solution.py:229
  43.1 7.2 %collective-permute-start.11 = (f32[384,128]{1,0:T(8,128)S(1)}, f32[384,128]{1,0:T(8,128)S(1)}, u32[]{:S(2)}, u32[]{:S(2)}) collective-permute-start(f32[384,128]{1,0:T(8,128)S(1)} %slice.25), channel_id=1, source_target_pairs={{0,1},{1,0},{2,3},{3,2},{4,5},{5,4},{6,7},{7,6},{8,9},{9,8},{10,11... | collective-permute-start | bytes 589832 | tf_op jit(solution)/shard_map/ppermute | solution.py:229
  50.4 5.7 %collective-permute-start.12 = (f32[320,128]{1,0:T(8,128)S(1)}, f32[320,128]{1,0:T(8,128)S(1)}, u32[]{:S(2)}, u32[]{:S(2)}) collective-permute-start(f32[320,128]{1,0:T(8,128)S(1)} %fusion), channel_id=1, source_target_pairs={{0,4},{1,5},{2,6},{3,7},{4,0},{5,1},{6,2},{7,3},{8,12},{9,13},{10,... | collective-permute-start | bytes 491528 | tf_op jit(solution)/shard_map/ppermute | solution.py:229
